TPU v7x, 256 devices: a whole 4x4x8 slice. The times are simulated.
256 devices in a mesh: rep: 4 (over x), fsdp: 64 (over y, z, core).
Axes of the slice: x: 4, y: 4, z: 8, core: 2. Of those that a mesh axis runs over, the one named last changes fastest.
Arguments:
- params: bfloat16 [2, 8192, 4608], P(None, 'fsdp'), may hold values from -6 to 6
- deltas: bfloat16 [4, 2, 8192, 4608], P('rep', None, 'fsdp'), may hold values from -3 to 3
- momentum: float32 [2, 8192, 4608], P(None, 'fsdp', 'rep'), may hold values from -2 to 2
Outputs:
- new_params: bfloat16 [2, 8192, 4608], P(None, 'fsdp')
- new_momentum: float32 [2, 8192, 4608], P(None, 'fsdp', 'rep')
All inputs are finite; a program needn't handle non-finite values.
Results may differ from a plain program's by a relative error of at most 0.0035.
Values may be sent and summed in bfloat16 or wider, within the bound.
No kernel may reach another device: no remote copies, remote signals or barrier semaphores. Data moves between devices by JAX's collectives and lax.ppermute only.
A program may use at most 64 MiB of HBM per device.

v0:
```python
import jax
import jax.numpy as jnp
from jax import lax
from jax.sharding import Mesh
from jax.sharding import PartitionSpec as P

Q_ROWS = 4096
KV_ROWS = 2048
FSDP = ("fsdp_0", "fsdp_1", "fsdp_2")
REP_FSDP = ("rep", "fsdp_0", "fsdp_1", "fsdp_2")


clip_share = 0.5
peak_eps = 1e-06
outer_rate = 0.7
momentum_decay = 0.9


def over_axes(value, axes):
    for axis in axes:
        value = lax.pmax(value, axis)
    return value


def cut_along(value, dim, count):
    before, after = (value.shape[:dim], value.shape[dim + 1 :])
    return jnp.moveaxis(value.reshape(*before, count, -1, *after), dim, 0)


def summed_on_arrival(value, axis, dim):
    count = lax.axis_size(axis)
    blocks = lax.all_to_all(cut_along(value, dim, count), axis, 0, 0, tiled=True)
    return jnp.sum(blocks.astype(jnp.float32), axis=0)


def from_everyone(value, axis):
    copies = jnp.broadcast_to(value, (lax.axis_size(axis), *value.shape))
    return lax.all_to_all(copies, axis, split_axis=0, concat_axis=0, tiled=True)


def laid_out(blocks, dim):
    shape = list(blocks.shape[1:])
    shape[dim] *= blocks.shape[0]
    return jnp.moveaxis(blocks, 0, dim).reshape(shape)


def collect(value, axis, dim):
    blocks = from_everyone(value, axis)
    return laid_out(blocks, dim)


def apply_update(summed, tau_rows, param_piece, moment, replicas):
    outer = tau_rows[..., None] * summed / jnp.float32(replicas)
    fresh_moment = momentum_decay * moment + outer
    fresh = (
        param_piece.astype(jnp.float32) - outer_rate * (outer + momentum_decay * fresh_moment)
    ).astype(jnp.bfloat16)
    return (fresh, fresh_moment)


def on_device(params, deltas, momentum):
    local = deltas[0]
    shard_rows = local.shape[1]
    row_ids = lax.axis_index(FSDP) * shard_rows + lax.iota(jnp.int32, shard_rows)
    tensor_ids = (row_ids >= Q_ROWS).astype(jnp.int32) + (row_ids >= Q_ROWS + KV_ROWS).astype(
        jnp.int32
    )
    member = tensor_ids[None, :] == lax.iota(jnp.int32, 3)[:, None]
    row_peak = jnp.max(jnp.abs(local), axis=2).astype(jnp.float32)
    local_peak = jnp.max(jnp.where(member[None], row_peak[:, None, :], jnp.float32(0.0)), axis=2)
    peak = over_axes(local_peak, REP_FSDP)
    scaled = clip_share * (peak + peak_eps)
    tau = jnp.sum(jnp.where(member[None], scaled[:, :, None], jnp.float32(0.0)), axis=1)
    codes = jnp.clip(local.astype(jnp.float32) / tau[..., None], -1.0, 1.0).astype(jnp.bfloat16)
    replicas = lax.axis_size("rep")
    owned = momentum.shape[2]
    start = lax.axis_index("rep") * owned
    param_piece = lax.dynamic_slice_in_dim(params, start, owned, 2)
    summed = summed_on_arrival(codes, "rep", 2)
    fresh, new_momentum = apply_update(summed, tau, param_piece, momentum, replicas)
    new_params = collect(fresh, "rep", 2)
    return (new_params, new_momentum)


def solution(mesh):
    torus = Mesh(
        mesh.devices.reshape(mesh.shape["rep"], 4, 8, 2), ("rep", "fsdp_0", "fsdp_1", "fsdp_2")
    )
    placed = (P(None, FSDP, None), P("rep", None, FSDP, None), P(None, FSDP, "rep"))
    return jax.shard_map(
        on_device,
        mesh=torus,
        in_specs=placed,
        out_specs=(P(None, FSDP, None), P(None, FSDP, "rep")),
        check_vma=False,
    )
```

profile of v0, /device:TPU:1, one launch (start us, length us, event | category | flops | bytes accessed | tf_op | source)
XLA Modules:
  0.0 130.2 jit_solution(16708686397631088744)
XLA Ops:
  0.7 2.2 %abs_reduce_fusion = bf16[2,128]{1,0:T(2,128)(2,1)S(1)} fusion(bf16[1,2,128,4608]{3,2,1,0:T(8,128)(2,1)} %param.4), kind=kLoop, calls=%fused_computation.5 | loop fusion | flops 2359040 | bytes 2359808 | tf_op jit(solution)/shard_map/reduce_max | solution.py:69
  2.9 0.1 select_reduce_fusion.1
  2.9 9.3 %pmax.28 = f32[2,3]{0,1:T(4,128)S(1)} all-reduce(f32[2,3]{0,1:T(4,128)S(1)} %select_reduce_fusion.1), channel_id=1, replica_groups=mesh['rep'=4,'fsdp_0'=4,'fsdp_1'=8,'fsdp_2'=2] {'rep'}, use_global_device_ids=true, to_apply=%region_2.3 | all-reduce | flops 6 | bytes 48 | tf_op jit(solution)/shard_map/pmax | solution.py:21
  12.2 9.0 %pmax.29 = f32[2,3]{0,1:T(4,128)S(1)} all-reduce(f32[2,3]{0,1:T(4,128)S(1)} %pmax.28), channel_id=1, replica_groups=mesh['rep'=4,'fsdp_0'=4,'fsdp_1'=8,'fsdp_2'=2] {'fsdp_0'}, use_global_device_ids=true, to_apply=%region_3.4 | all-reduce | flops 6 | bytes 48 | tf_op jit(solution)/shard_map/pmax | solution.py:21
  21.2 16.2 %pmax.30 = f32[2,3]{0,1:T(4,128)S(1)} all-reduce(f32[2,3]{0,1:T(4,128)S(1)} %pmax.29), channel_id=1, replica_groups=mesh['rep'=4,'fsdp_0'=4,'fsdp_1'=8,'fsdp_2'=2] {'fsdp_1'}, use_global_device_ids=true, to_apply=%region_4.5 | all-reduce | flops 6 | bytes 48 | tf_op jit(solution)/shard_map/pmax | solution.py:21
  37.4 3.0 %copy.9 = bf16[1,2,128,4608]{2,3,1,0:T(8,128)(2,1)S(1)} copy(bf16[1,2,128,4608]{3,2,1,0:T(8,128)(2,1)} %param.4) | data formatting | bytes 4718592 | tf_op args[1]
  40.4 10.4 %pmax.31 = f32[2,3]{0,1:T(4,128)S(1)} all-reduce(f32[2,3]{0,1:T(4,128)S(1)} %pmax.30), channel_id=1, replica_groups=mesh['rep'=4,'fsdp_0'=4,'fsdp_1'=8,'fsdp_2'=2] {'fsdp_2'}, use_global_device_ids=true, to_apply=%region_5.6 | all-reduce | flops 6 | bytes 48 | tf_op jit(solution)/shard_map/pmax | solution.py:21
  50.8 0.1 select_reduce_fusion
  50.9 2.0 %fusion.2 = bf16[4,2,128,1152]{2,3,0,1:T(8,128)(2,1)} fusion(bf16[2,128,4,1152]{1,3,2,0:T(8,128)(2,1)S(1)} %bitcast.7, f32[2,128]{1,0:T(2,128)S(1)} %select_reduce_fusion), kind=kLoop, calls=%fused_computation.4 | loop fusion | flops 4718592 | bytes 4719616 | tf_op jit(solution)/shard_map/transpose | solution.py:27
  52.9 4.3 %copy.10 = bf16[4,2,128,1152]{3,2,1,0:T(8,128)(2,1)} copy(bf16[4,2,128,1152]{2,3,0,1:T(8,128)(2,1)} %fusion.2) | data formatting | bytes 4718592 | tf_op jit(solution)/shard_map/transpose | solution.py:27
  57.2 3.6 %all-to-all-start = ((bf16[4,2,128,1152]{3,2,1,0:T(8,128)(2,1)}), bf16[4,2,128,1152]{3,2,1,0:T(8,128)(2,1)S(1)}, u32[]{:S(2)}, u32[]{:S(2)}) async-start(bf16[4,2,128,1152]{3,2,1,0:T(8,128)(2,1)} %copy.10), calls=%async_computation | async-start | bytes 4718592 | tf_op jit(solution)/shard_map/all_to_all | solution.py:32
  60.9 0.0 copy-start
  60.9 28.8 %all-to-all-done = bf16[4,2,128,1152]{3,2,1,0:T(8,128)(2,1)S(1)} async-done(((bf16[4,2,128,1152]{3,2,1,0:T(8,128)(2,1)}), bf16[4,2,128,1152]{3,2,1,0:T(8,128)(2,1)S(1)}, u32[]{:S(2)}, u32[]{:S(2)}) %all-to-all-start) | async-done | bytes 2359328 | tf_op jit(solution)/shard_map/all_to_all | solution.py:32
  89.7 0.3 convert_reduce_fusion
  90.1 0.0 copy-done
  90.1 2.5 %subtract_convert_fusion = (bf16[2,128,1152]{2,1,0:T(8,128)(2,1)S(1)}, f32[2,128,1152]{2,1,0:T(8,128)}) fusion(f32[2,128,1152]{2,1,0:T(8,128)S(1)} %convert_reduce_fusion, f32[2,128]{1,0:T(2,128)S(1)} %select_reduce_fusion, bf16[2,128,4608]{2,1,0:T(8,128)(2,1)} %param.3, s32[]{:T(128)S(6)} %select_n.11, f32[2,128,1152]{2,1,0:T(8,128)S(1)} %copy-done), kind=kLoop, calls=%fused_computation.6 | loop fusion | flops 2949120 | bytes 4719620 | tf_op jit(solution)/shard_map/convert_element_type | solution.py:57
  92.6 0.3 broadcast_in_dim.51
  92.9 30.5 %all_to_all.10 = bf16[4,2,128,1152]{3,2,1,0:T(8,128)(2,1)S(1)} all-to-all(bf16[4,2,128,1152]{3,2,1,0:T(8,128)(2,1)S(1)} %broadcast_in_dim.51), channel_id=1, replica_groups=mesh['rep'=4,'fsdp_0'=4,'fsdp_1'=8,'fsdp_2'=2] {'rep'}, dimensions={0} | all-to-all | bytes 4718592 | tf_op jit(solution)/shard_map/all_to_all | solution.py:38
  123.4 2.5 %copy.11 = bf16[4,2,128,1152]{2,3,0,1:T(8,128)(2,1)} copy(bf16[4,2,128,1152]{3,2,1,0:T(8,128)(2,1)S(1)} %all_to_all.10) | data formatting | bytes 4718592 | tf_op jit(solution)/shard_map/all_to_all | solution.py:38
  125.9 4.3 %copy.12 = bf16[2,128,4608]{2,1,0:T(8,128)(2,1)} copy(bf16[2,128,4608]{1,2,0:T(8,128)(2,1)} %bitcast.8) | data formatting | bytes 4718592
  (4 shorter events, 0.0 us)
Async XLA Ops:
  57.2 32.5 %all-to-all-start = ((bf16[4,2,128,1152]{3,2,1,0:T(8,128)(2,1)}), bf16[4,2,128,1152]{3,2,1,0:T(8,128)(2,1)S(1)}, u32[]{:S(2)}, u32[]{:S(2)}) async-start(bf16[4,2,128,1152]{3,2,1,0:T(8,128)(2,1)} %copy.10), calls=%async_computation | async-start | bytes 4718592 | tf_op jit(solution)/shard_map/all_to_all | solution.py:32
  60.9 29.2 %copy-start = (f32[2,128,1152]{2,1,0:T(8,128)S(1)}, f32[2,128,1152]{2,1,0:T(8,128)}, u32[]{:S(2)}) copy-start(f32[2,128,1152]{2,1,0:T(8,128)} %param.5) | copy-start | bytes 3538948
where the time goes:
time: 131 us; the launch traced here: 130 us
  blocking collectives  75.3 us (57%)
  waiting for transfers between devices  28.8 us (22%)
  local copies, waits for them, and re-layouts  14.5 us (11%)
  other arithmetic  7.26 us (6%)
  starting transfers between devices  3.63 us (3%)
    pmax x4, blocking collectives, over_axes(): value = lax.pmax(value, axis)  44.8 us
    all_to_all x1, blocking collectives, from_everyone(): return lax.all_to_all(copies, axis, split_axis=0, concat_axis=0, tiled=True)  30.5 us
    all_to_all x1, waiting for transfers between devices, summed_on_arrival(): lax.all_to_all(cut_along(value, dim, count), axis, 0, 0, tiled=True)  28.8 us
    unnamed x4, local copies, waits for them, and re-layouts  7.31 us
    transpose x1, local copies, waits for them, and re-layouts, cut_along(): return jnp.moveaxis(value.reshape(*before, count, -1, *after), dim, 0)  4.34 us
    all_to_all x1, starting transfers between devices, summed_on_arrival(): lax.all_to_all(cut_along(value, dim, count), axis, 0, 0, tiled=True)  3.63 us
  transfers between devices with their start and end apart: 1, of which 1 were waited for; matrix products, arithmetic and copies ran while one was open for 0% of the time, Pallas kernels for 0%

commit v1 on v0

v1 whole, which is shorter than its diff:
```python
import functools

import jax
import jax.numpy as jnp
from jax import lax
from jax.experimental import pallas as pl
from jax.experimental.pallas import tpu as pltpu
from jax.sharding import Mesh
from jax.sharding import PartitionSpec as P


Q_ROWS = 4096
KV_ROWS = 2048
FSDP = ("fsdp_0", "fsdp_1", "fsdp_2")
REP = 4

clip_share = 0.5
peak_eps = 1e-06
outer_rate = 0.7
momentum_decay = 0.9


def part_kernel(me_ref, local_ref, b2_ref, b1_ref, b3_ref, top_ref):
    owned = b1_ref.shape[2]
    me = me_ref[0]
    step = local_ref.shape[1]
    first = pl.multiple_of(pl.program_id(0) * step, step)
    for ahead, ref in ((2, b2_ref), (1, b1_ref), (3, b3_ref)):
        start = pl.multiple_of(lax.rem(me + ahead, REP) * owned, 128)
        ref[:, pl.ds(first, step), :] = local_ref[:, :, pl.ds(start, owned)]
    size = jnp.max(jnp.abs(local_ref[...]).astype(jnp.float32), axis=2, keepdims=True)
    size = jnp.max(size, axis=1)

    @pl.when(pl.program_id(0) == 0)
    def _():
        top_ref[...] = jnp.zeros_like(top_ref)

    top_ref[...] = jnp.maximum(top_ref[...], jnp.broadcast_to(size, top_ref.shape))


def parts_and_top(local, me, owned):
    layers, rows, width = local.shape
    step = 32
    block = pl.BlockSpec(memory_space=pltpu.VMEM)
    piece = jax.ShapeDtypeStruct((layers, rows, owned), local.dtype)
    return pl.pallas_call(
        part_kernel,
        grid_spec=pltpu.PrefetchScalarGridSpec(
            num_scalar_prefetch=1,
            grid=(rows // step,),
            in_specs=[pl.BlockSpec((layers, step, width), lambda i, me: (0, i, 0))],
            out_specs=[block, block, block, pl.BlockSpec((layers, 128), lambda i, me: (0, 0))],
        ),
        out_shape=[piece, piece, piece, jax.ShapeDtypeStruct((layers, 128), jnp.float32)],
        name="parts_and_top",
    )(me, local)


def update_kernel(layer, me_ref, tau_ref, own_ref, r2_ref, r1_ref, r3_ref, p_ref, m_ref, *rest):
    fresh_ref, new_ref = rest[-2:]
    tau = tau_ref[layer]
    inverse = tau_ref[layer + 2]
    total = None
    step = own_ref.shape[1]
    here = pl.ds(pl.multiple_of(pl.program_id(0) * step, step), step)
    blocks = (own_ref[0], r1_ref[layer, here], r2_ref[layer, here], r3_ref[layer, here])
    for block in blocks:
        code = jnp.clip(block.astype(jnp.float32) * inverse, -1.0, 1.0)
        code = code.astype(jnp.bfloat16).astype(jnp.float32)
        total = code if total is None else total + code
    outer = (tau / REP) * total
    fresh_moment = momentum_decay * m_ref[0] + outer
    fresh = p_ref[0].astype(jnp.float32) - outer_rate * (outer + momentum_decay * fresh_moment)
    fresh_ref[here] = fresh.astype(jnp.bfloat16)
    new_ref[0] = fresh_moment


def update(layer, me, tau, local, received, params, momentum, earlier):
    _, rows, owned = momentum.shape
    step = 32
    mine = pl.BlockSpec((1, step, owned), lambda i, me, tau: (layer, i, me[0]))
    flat = pl.BlockSpec((1, step, owned), lambda i, me, tau: (layer, i, 0))
    operands = [local, *received, params, momentum]
    whole = pl.BlockSpec(memory_space=pltpu.VMEM)
    specs = [mine, whole, whole, whole, mine, flat]
    aliases = {}
    if earlier is not None:
        operands.append(earlier)
        specs.append(pl.BlockSpec(memory_space=pl.ANY))
        aliases = {len(operands) + 1: 1}
    return pl.pallas_call(
        functools.partial(update_kernel, layer),
        grid_spec=pltpu.PrefetchScalarGridSpec(
            num_scalar_prefetch=2,
            grid=(rows // step,),
            in_specs=specs,
            out_specs=[whole, flat],
        ),
        out_shape=[
            jax.ShapeDtypeStruct((rows, owned), jnp.bfloat16),
            jax.ShapeDtypeStruct(momentum.shape, jnp.float32),
        ],
        input_output_aliases=aliases,
    )(me, tau, *operands)


def place_kernel(moves, me_ref, *refs):
    sems = refs[-1]
    out_ref = refs[-2]
    copies = []
    for k, (layer, back, first, count) in enumerate(moves):
        src = refs[k]
        owned = src.shape[-1]
        start = pl.multiple_of(lax.rem(me_ref[0] + back, REP) * owned, 128)
        dst = out_ref.at[layer, pl.ds(first, count), pl.ds(start, owned)]
        copies.append(pltpu.make_async_copy(src, dst, sems.at[k]))
    for copy in copies:
        copy.start()
    for copy in copies:
        copy.wait()


def place(me, moves, pieces, shape, earlier):
    operands = list(pieces)
    aliases = {}
    if earlier is not None:
        operands.append(earlier)
        aliases = {len(operands): 0}
    return pl.pallas_call(
        functools.partial(place_kernel, moves),
        in_specs=[pl.BlockSpec(memory_space=pltpu.SMEM)]
        + [pl.BlockSpec(memory_space=pltpu.VMEM)] * len(pieces)
        + [pl.BlockSpec(memory_space=pl.ANY)] * len(aliases),
        out_specs=pl.BlockSpec(memory_space=pl.ANY),
        out_shape=jax.ShapeDtypeStruct(shape, jnp.bfloat16),
        scratch_shapes=[pltpu.SemaphoreType.DMA((len(moves),))],
        input_output_aliases=aliases,
        name="place",
    )(me, *operands)


def spread(value, axes):
    copies = jnp.broadcast_to(value, (lax.axis_size(axes), *value.shape))
    return lax.all_to_all(copies, axes, 0, 0, tiled=True)


def tensor_of(y, rows):
    first = y * (16 * rows)
    return (first >= Q_ROWS).astype(jnp.int32) + (first >= Q_ROWS + KV_ROWS).astype(jnp.int32)


def shift(value, by):
    return lax.ppermute(value, "rep", [(i, (i + by) % REP) for i in range(REP)])


def on_device(params, deltas, momentum):
    local = deltas[0]
    _, rows, owned = momentum.shape
    me = lax.axis_index("rep").reshape(1)
    b2, b1, b3, top = parts_and_top(local, me, owned)
    r2 = shift(b2, 2)
    r1 = shift(b1, 1)
    r3 = shift(b3, 3)
    top = jnp.max(spread(top[:, 0], ("fsdp_1", "fsdp_2")), axis=0)
    tops = spread(top, ("rep", "fsdp_0"))
    ys = lax.rem(lax.iota(jnp.int32, 16), 4)
    same = (tensor_of(ys, rows) == tensor_of(lax.axis_index("fsdp_0"), rows))[:, None]
    tau = clip_share * (jnp.max(jnp.where(same, tops, 0.0), axis=0) + peak_eps)
    tau = jnp.concatenate([tau, 1.0 / tau])
    received = (r2, r1, r3)
    fresh0, new_m = update(0, me, tau, local, received, params, momentum, None)
    right0, left0 = shift(fresh0, 1), shift(fresh0, 3)
    fresh1, new_m = update(1, me, tau, local, received, params, momentum, new_m)
    right1, left1 = shift(fresh1, 1), shift(fresh1, 3)
    half = rows // 2
    far0 = (shift(right0[:half], 1), shift(left0[half:], 3))
    far1 = (shift(right1[:half], 1), shift(left1[half:], 3))
    moves = [(l, b, 0, rows) for l in range(2) for b in (0, 3, 1)]
    out = place(me, moves, (fresh0, right0, left0, fresh1, right1, left1), params.shape, None)
    moves = [(l, 2, f, half) for l in range(2) for f in (0, half)]
    out = place(me, moves, (*far0, *far1), params.shape, out)
    return out, new_m


def solution(mesh):
    torus = Mesh(
        mesh.devices.reshape(mesh.shape["rep"], 4, 8, 2), ("rep", "fsdp_0", "fsdp_1", "fsdp_2")
    )
    placed = (P(None, FSDP, None), P("rep", None, FSDP, None), P(None, FSDP, "rep"))
    return jax.shard_map(
        on_device,
        mesh=torus,
        in_specs=placed,
        out_specs=(P(None, FSDP, None), P(None, FSDP, "rep")),
        check_vma=False,
    )
```

time: 131 us -> 80.5 us (0.61)
  the two profiles are of different devices: /device:TPU:1 before, /device:TPU:8 now
where the time goes in v1:
time: 80.5 us; the launch traced here: 80 us
  starting transfers between devices  28.6 us (36%)
  waiting for transfers between devices  26.6 us (33%)
  Pallas kernels  18.7 us (23%)
  local copies, waits for them, and re-layouts  4.56 us (6%)
  other arithmetic  0.82 us (1%)
    ppermute x11, starting transfers between devices, shift(): return lax.ppermute(value, 'rep', [(i, (i + by) % REP) for i in range(REP)])  15.1 us
    all_to_all x2, waiting for transfers between devices, spread(): return lax.all_to_all(copies, axes, 0, 0, tiled=True)  13.8 us
    all_to_all x2, starting transfers between devices, spread(): return lax.all_to_all(copies, axes, 0, 0, tiled=True)  13.5 us
    ppermute x11, waiting for transfers between devices, shift(): return lax.ppermute(value, 'rep', [(i, (i + by) % REP) for i in range(REP)])  12.7 us
    pallas_call x2, Pallas kernels, update(): pl.pallas_call(functools.partial(update_kernel, layer), grid_spec=pltpu.P...  10.2 us
    pallas_call x2, Pallas kernels, place(): pl.pallas_call(functools.partial(place_kernel, moves), in_specs=[pl.Block...  4.62 us
    pallas_call x1, Pallas kernels, parts_and_top(): pl.pallas_call(part_kernel, grid_spec=pltpu.PrefetchScalarGridSpec(num_sc...  3.95 us
    unnamed x24, local copies, waits for them, and re-layouts  2.48 us
  transfers between devices with their start and end apart: 13, of which 6 were waited for; matrix products, arithmetic and copies ran while one was open for 4% of the time, Pallas kernels for 3%

profile of v1, /device:TPU:8, one launch (start us, length us, event | category | flops | bytes accessed | tf_op | source)
XLA Modules:
  0.0 80.0 jit_solution(774094412924285520)
XLA Ops:
  0.6 3.9 %parts_and_top.1 = (bf16[2,128,1152]{2,1,0:T(8,128)(2,1)}, bf16[2,128,1152]{2,1,0:T(8,128)(2,1)}, bf16[2,128,1152]{2,1,0:T(8,128)(2,1)}, f32[2,128]{1,0:T(2,128)}) custom-call(s32[1]{0:T(128)} %bitcast.me_ref, bf16[2,128,4608]{2,1,0:T(8,128)(2,1)} %bitcast.6), custom_call_target="tpu_custom_call" | custom-call | tf_op jit(solution)/shard_map/parts_and_top/pallas_call | solution.py:46
  4.6 3.0 %collective-permute-start = (bf16[2,128,1152]{2,1,0:T(8,128)(2,1)}, bf16[2,128,1152]{2,1,0:T(8,128)(2,1)S(1)}, u32[]{:S(2)}, u32[]{:S(2)}) collective-permute-start(bf16[2,128,1152]{2,1,0:T(8,128)(2,1)} %get-tuple-element.11), channel_id=1, source_target_pairs={{0,128},{64,192},{128,0},{192,64},{1,129},{65,193},{129,1},{193,65... | collective-permute-start | bytes 1769480 | tf_op jit(solution)/shard_map/ppermute | solution.py:153
  7.6 0.6 collective-permute-start.1
  8.2 2.6 %collective-permute-start.2 = (bf16[2,128,1152]{2,1,0:T(8,128)(2,1)}, bf16[2,128,1152]{2,1,0:T(8,128)(2,1)S(1)}, u32[]{:S(2)}, u32[]{:S(2)}) collective-permute-start(bf16[2,128,1152]{2,1,0:T(8,128)(2,1)} %get-tuple-element.13), channel_id=1, source_target_pairs={{0,192},{64,0},{128,64},{192,128},{1,193},{65,1},{129,65},{193,129... | collective-permute-start | bytes 1769480 | tf_op jit(solution)/shard_map/ppermute | solution.py:153
  10.8 0.7 slice_reduce_fusion
  11.6 0.6 broadcast_in_dim.23
  12.2 8.6 %all-to-all-start = ((f32[16,1,2]{2,1,0:T(1,128)}), f32[16,1,2]{2,1,0:T(1,128)S(1)}, u32[]{:S(2)}, u32[]{:S(2)}) async-start(f32[16,1,2]{2,1,0:T(1,128)} %broadcast_in_dim.23), calls=%async_computation | async-start | bytes 16384 | tf_op jit(solution)/shard_map/all_to_all | solution.py:144
  20.8 7.6 %all-to-all-done = f32[16,1,2]{2,1,0:T(1,128)S(1)} async-done(((f32[16,1,2]{2,1,0:T(1,128)}), f32[16,1,2]{2,1,0:T(1,128)S(1)}, u32[]{:S(2)}, u32[]{:S(2)}) %all-to-all-start) | async-done | bytes 160 | tf_op jit(solution)/shard_map/all_to_all | solution.py:144
  28.4 0.6 broadcast_in_dim.24
  29.0 4.9 %all-to-all-start.1 = ((f32[16,1,2]{2,1,0:T(1,128)}), f32[16,1,2]{2,1,0:T(1,128)S(1)}, u32[]{:S(2)}, u32[]{:S(2)}) async-start(f32[16,1,2]{2,1,0:T(1,128)} %broadcast_in_dim.24), calls=%async_computation.1 | async-start | bytes 16384 | tf_op jit(solution)/shard_map/all_to_all | solution.py:144
  34.0 6.2 %all-to-all-done.1 = f32[16,1,2]{2,1,0:T(1,128)S(1)} async-done(((f32[16,1,2]{2,1,0:T(1,128)}), f32[16,1,2]{2,1,0:T(1,128)S(1)}, u32[]{:S(2)}, u32[]{:S(2)}) %all-to-all-start.1) | async-done | bytes 160 | tf_op jit(solution)/shard_map/all_to_all | solution.py:144
  40.2 0.1 copy.10
  40.3 0.1 fusion
  40.4 0.6 pad_maximum_fusion.tau_ref
  41.0 0.0 collective-permute-done.r2_ref
  41.0 0.0 copy-start
  41.0 0.0 collective-permute-done.1.r1_ref
  41.0 0.0 copy-start.1
  41.1 0.0 collective-permute-done.2.r3_ref
  41.1 0.8 %copy-done = bf16[2,128,1152]{2,1,0:T(8,128)(2,1)} copy-done((bf16[2,128,1152]{2,1,0:T(8,128)(2,1)}, bf16[2,128,1152]{2,1,0:T(8,128)(2,1)S(1)}, u32[]{:S(2)}) %copy-start) | copy-done | bytes 589848
  41.9 0.2 copy-done.1
  42.1 0.0 copy-start.2
  42.1 0.8 %copy-done.2 = bf16[2,128,1152]{2,1,0:T(8,128)(2,1)} copy-done((bf16[2,128,1152]{2,1,0:T(8,128)(2,1)}, bf16[2,128,1152]{2,1,0:T(8,128)(2,1)S(1)}, u32[]{:S(2)}) %copy-start.2) | copy-done | bytes 589848
  42.9 5.0 %shard_map.50 = (bf16[128,1152]{1,0:T(8,128)(2,1)}, f32[2,128,1152]{2,1,0:T(8,128)}) custom-call(s32[1]{0:T(128)} %bitcast.me_ref, f32[4]{0:T(128)} %pad_maximum_fusion.tau_ref, bf16[2,128,4608]{2,1,0:T(8,128)(2,1)} %bitcast.7, bf16[2,128,1152]{2,1,0:T(8,128)(2,1)} %copy-done, bf16[2,128,1152]{2,1,0:T(8,128)(2,1)} %copy-done.1, ...), custom_call_target="tpu_custom_call" | custom-call | tf_op jit(solution)/shard_map/pallas_call | solution.py:91
  47.9 0.0 copy-start.7
  47.9 5.2 %shard_map.51 = (bf16[128,1152]{1,0:T(8,128)(2,1)}, f32[2,128,1152]{2,1,0:T(8,128)}) custom-call(s32[1]{0:T(128)} %bitcast.me_ref, f32[4]{0:T(128)} %pad_maximum_fusion.tau_ref, bf16[2,128,4608]{2,1,0:T(8,128)(2,1)} %bitcast.8, bf16[2,128,1152]{2,1,0:T(8,128)(2,1)} %copy-done, bf16[2,128,1152]{2,1,0:T(8,128)(2,1)} %copy-done.1, ...), custom_call_target="tpu_custom_call", output_to_operand_aliasing={{1}: (8, {})} | custom-call | tf_op jit(solution)/shard_map/pallas_call | solution.py:91
  53.0 1.0 %collective-permute-start.9 = (bf16[128,1152]{1,0:T(8,128)(2,1)}, bf16[128,1152]{1,0:T(8,128)(2,1)S(1)}, u32[]{:S(2)}, u32[]{:S(2)}) collective-permute-start(bf16[128,1152]{1,0:T(8,128)(2,1)} %get-tuple-element.16.refs_3_), channel_id=1, source_target_pairs={{0,192},{64,0},{128,64},{192,128},{1,193},{65,1},{129,65},{193,129... | collective-permute-start | bytes 884744 | tf_op jit(solution)/shard_map/ppermute | solution.py:153
  54.1 1.0 %collective-permute-start.7 = (bf16[128,1152]{1,0:T(8,128)(2,1)}, bf16[128,1152]{1,0:T(8,128)(2,1)S(1)}, u32[]{:S(2)}, u32[]{:S(2)}) collective-permute-start(bf16[128,1152]{1,0:T(8,128)(2,1)} %get-tuple-element.16.refs_3_), channel_id=1, source_target_pairs={{0,64},{64,128},{128,192},{192,0},{1,65},{65,129},{129,193},{193,1... | collective-permute-start | bytes 884744 | tf_op jit(solution)/shard_map/ppermute | solution.py:153
  55.1 0.0 copy-done.7
  55.1 2.2 %collective-permute-start.5 = (bf16[128,1152]{1,0:T(8,128)(2,1)S(1)}, bf16[128,1152]{1,0:T(8,128)(2,1)S(1)}, u32[]{:S(2)}, u32[]{:S(2)}) collective-permute-start(bf16[128,1152]{1,0:T(8,128)(2,1)S(1)} %copy-done.7), channel_id=1, source_target_pairs={{0,192},{64,0},{128,64},{192,128},{1,193},{65,1},{129,65},{193,129... | collective-permute-start | bytes 884744 | tf_op jit(solution)/shard_map/ppermute | solution.py:153
  57.3 0.0 collective-permute-start.3
  57.3 5.8 %collective-permute-done.9.refs_5_ = bf16[128,1152]{1,0:T(8,128)(2,1)S(1)} collective-permute-done((bf16[128,1152]{1,0:T(8,128)(2,1)}, bf16[128,1152]{1,0:T(8,128)(2,1)S(1)}, u32[]{:S(2)}, u32[]{:S(2)}) %collective-permute-start.9) | collective-permute-done | bytes 294944 | tf_op jit(solution)/shard_map/ppermute | solution.py:153
  63.1 0.0 copy-start.3
  63.2 2.3 %collective-permute-start.10 = (bf16[64,1152]{1,0:T(8,128)(2,1)S(1)}, bf16[64,1152]{1,0:T(8,128)(2,1)S(1)}, u32[]{:S(2)}, u32[]{:S(2)}) collective-permute-start(bf16[64,1152]{1,0:T(8,128)(2,1)S(1)} %slice.23), channel_id=1, source_target_pairs={{0,192},{64,0},{128,64},{192,128},{1,193},{65,1},{129,65},{193,129... | collective-permute-start | bytes 442376 | tf_op jit(solution)/shard_map/ppermute | solution.py:153
  65.5 0.0 collective-permute-done.7.refs_4_
  65.5 0.0 copy-start.4
  65.5 0.1 collective-permute-start.8
  65.6 3.9 %collective-permute-done.5.refs_2_ = bf16[128,1152]{1,0:T(8,128)(2,1)S(1)} collective-permute-done((bf16[128,1152]{1,0:T(8,128)(2,1)S(1)}, bf16[128,1152]{1,0:T(8,128)(2,1)S(1)}, u32[]{:S(2)}, u32[]{:S(2)}) %collective-permute-start.5) | collective-permute-done | bytes 294944 | tf_op jit(solution)/shard_map/ppermute | solution.py:153
  69.5 0.0 copy-start.5
  69.5 1.5 %collective-permute-start.6 = (bf16[64,1152]{1,0:T(8,128)(2,1)S(1)}, bf16[64,1152]{1,0:T(8,128)(2,1)S(1)}, u32[]{:S(2)}, u32[]{:S(2)}) collective-permute-start(bf16[64,1152]{1,0:T(8,128)(2,1)S(1)} %slice.21), channel_id=1, source_target_pairs={{0,192},{64,0},{128,64},{192,128},{1,193},{65,1},{129,65},{193,129... | collective-permute-start | bytes 442376 | tf_op jit(solution)/shard_map/ppermute | solution.py:153
  71.0 0.0 collective-permute-done.3.refs_1_
  71.0 0.0 copy-start.6
  71.0 0.7 collective-permute-start.4
  71.7 0.0 copy-done.3
  71.7 0.0 copy-done.4
  71.7 0.0 copy-done.5
  71.7 0.0 copy-done.6
  71.7 2.7 %place.2.refs_4_ = bf16[2,128,4608]{2,1,0:T(8,128)(2,1)} custom-call(s32[1]{0:T(128)} %bitcast.me_ref, bf16[128,1152]{1,0:T(8,128)(2,1)} %get-tuple-element.14.refs_0_, bf16[128,1152]{1,0:T(8,128)(2,1)} %copy-done.6, bf16[128,1152]{1,0:T(8,128)(2,1)} %copy-done.5, bf16[128,1152]{1,0:T(8,128)(2,1)} %get-tuple-element.16.refs_3_, bf16[128,1152]{1,0:T(8,128)(2,1)} %copy-done.4, ...), custom_call_target="tpu_custom_call" | custom-call | tf_op jit(solution)/shard_map/place/pallas_call | solution.py:129
  74.4 0.0 collective-permute-done.10.refs_3_
  74.4 0.0 copy-start.8
  74.4 0.0 collective-permute-done.8.refs_2_
  74.4 0.0 copy-start.9
  74.4 0.3 collective-permute-done.6.refs_1_
  74.7 0.0 copy-start.10
  74.7 2.7 %collective-permute-done.4.refs_0_ = bf16[64,1152]{1,0:T(8,128)(2,1)S(1)} collective-permute-done((bf16[64,1152]{1,0:T(8,128)(2,1)S(1)}, bf16[64,1152]{1,0:T(8,128)(2,1)S(1)}, u32[]{:S(2)}, u32[]{:S(2)}) %collective-permute-start.4) | collective-permute-done | bytes 147488 | tf_op jit(solution)/shard_map/ppermute | solution.py:153
  77.4 0.0 copy-done.8
  77.4 0.0 copy-done.9
  77.4 0.0 copy-done.10
  77.4 0.0 copy-start.11
  77.4 0.7 copy-done.11
  78.1 2.0 %place.3 = bf16[2,128,4608]{2,1,0:T(8,128)(2,1)} custom-call(s32[1]{0:T(128)} %bitcast.me_ref, bf16[64,1152]{1,0:T(8,128)(2,1)} %copy-done.11, bf16[64,1152]{1,0:T(8,128)(2,1)} %copy-done.10, bf16[64,1152]{1,0:T(8,128)(2,1)} %copy-done.9, bf16[64,1152]{1,0:T(8,128)(2,1)} %copy-done.8, bf16[2,128,4608]{2,1,0:T(8,128)(2,1)} %place.2.refs_4_), custom_call_target="tpu_custom_call", output_to_operand_aliasing={{}: (5, {})} | custom-call | tf_op jit(solution)/shard_map/place/pallas_call | solution.py:129
  (7 shorter events, 0.1 us)
Async XLA Ops:
  4.6 36.5 %collective-permute-start = (bf16[2,128,1152]{2,1,0:T(8,128)(2,1)}, bf16[2,128,1152]{2,1,0:T(8,128)(2,1)S(1)}, u32[]{:S(2)}, u32[]{:S(2)}) collective-permute-start(bf16[2,128,1152]{2,1,0:T(8,128)(2,1)} %get-tuple-element.11), channel_id=1, source_target_pairs={{0,128},{64,192},{128,0},{192,64},{1,129},{65,193},{129,1},{193,65... | collective-permute-start | bytes 1769480 | tf_op jit(solution)/shard_map/ppermute | solution.py:153
  7.6 33.4 %collective-permute-start.1 = (bf16[2,128,1152]{2,1,0:T(8,128)(2,1)}, bf16[2,128,1152]{2,1,0:T(8,128)(2,1)S(1)}, u32[]{:S(2)}, u32[]{:S(2)}) collective-permute-start(bf16[2,128,1152]{2,1,0:T(8,128)(2,1)} %get-tuple-element.12), channel_id=1, source_target_pairs={{0,64},{64,128},{128,192},{192,0},{1,65},{65,129},{129,193},{193,1... | collective-permute-start | bytes 1769480 | tf_op jit(solution)/shard_map/ppermute | solution.py:153
  8.2 32.9 %collective-permute-start.2 = (bf16[2,128,1152]{2,1,0:T(8,128)(2,1)}, bf16[2,128,1152]{2,1,0:T(8,128)(2,1)S(1)}, u32[]{:S(2)}, u32[]{:S(2)}) collective-permute-start(bf16[2,128,1152]{2,1,0:T(8,128)(2,1)} %get-tuple-element.13), channel_id=1, source_target_pairs={{0,192},{64,0},{128,64},{192,128},{1,193},{65,1},{129,65},{193,129... | collective-permute-start | bytes 1769480 | tf_op jit(solution)/shard_map/ppermute | solution.py:153
  12.2 16.2 %all-to-all-start = ((f32[16,1,2]{2,1,0:T(1,128)}), f32[16,1,2]{2,1,0:T(1,128)S(1)}, u32[]{:S(2)}, u32[]{:S(2)}) async-start(f32[16,1,2]{2,1,0:T(1,128)} %broadcast_in_dim.23), calls=%async_computation | async-start | bytes 16384 | tf_op jit(solution)/shard_map/all_to_all | solution.py:144
  29.0 11.2 %all-to-all-start.1 = ((f32[16,1,2]{2,1,0:T(1,128)}), f32[16,1,2]{2,1,0:T(1,128)S(1)}, u32[]{:S(2)}, u32[]{:S(2)}) async-start(f32[16,1,2]{2,1,0:T(1,128)} %broadcast_in_dim.24), calls=%async_computation.1 | async-start | bytes 16384 | tf_op jit(solution)/shard_map/all_to_all | solution.py:144
  41.0 0.8 %copy-start = (bf16[2,128,1152]{2,1,0:T(8,128)(2,1)}, bf16[2,128,1152]{2,1,0:T(8,128)(2,1)S(1)}, u32[]{:S(2)}) copy-start(bf16[2,128,1152]{2,1,0:T(8,128)(2,1)S(1)} %collective-permute-done.r2_ref) | copy-start | bytes 1769476
  41.0 1.0 %copy-start.1 = (bf16[2,128,1152]{2,1,0:T(8,128)(2,1)}, bf16[2,128,1152]{2,1,0:T(8,128)(2,1)S(1)}, u32[]{:S(2)}) copy-start(bf16[2,128,1152]{2,1,0:T(8,128)(2,1)S(1)} %collective-permute-done.1.r1_ref) | copy-start | bytes 1769476
  42.1 0.8 %copy-start.2 = (bf16[2,128,1152]{2,1,0:T(8,128)(2,1)}, bf16[2,128,1152]{2,1,0:T(8,128)(2,1)S(1)}, u32[]{:S(2)}) copy-start(bf16[2,128,1152]{2,1,0:T(8,128)(2,1)S(1)} %collective-permute-done.2.r3_ref) | copy-start | bytes 1769476
  47.9 7.2 %copy-start.7 = (bf16[128,1152]{1,0:T(8,128)(2,1)S(1)}, bf16[128,1152]{1,0:T(8,128)(2,1)}, u32[]{:S(2)}) copy-start(bf16[128,1152]{1,0:T(8,128)(2,1)} %get-tuple-element.14.refs_0_) | copy-start | bytes 884740
  53.0 10.1 %collective-permute-start.9 = (bf16[128,1152]{1,0:T(8,128)(2,1)}, bf16[128,1152]{1,0:T(8,128)(2,1)S(1)}, u32[]{:S(2)}, u32[]{:S(2)}) collective-permute-start(bf16[128,1152]{1,0:T(8,128)(2,1)} %get-tuple-element.16.refs_3_), channel_id=1, source_target_pairs={{0,192},{64,0},{128,64},{192,128},{1,193},{65,1},{129,65},{193,129... | collective-permute-start | bytes 884744 | tf_op jit(solution)/shard_map/ppermute | solution.py:153
  54.1 11.4 %collective-permute-start.7 = (bf16[128,1152]{1,0:T(8,128)(2,1)}, bf16[128,1152]{1,0:T(8,128)(2,1)S(1)}, u32[]{:S(2)}, u32[]{:S(2)}) collective-permute-start(bf16[128,1152]{1,0:T(8,128)(2,1)} %get-tuple-element.16.refs_3_), channel_id=1, source_target_pairs={{0,64},{64,128},{128,192},{192,0},{1,65},{65,129},{129,193},{193,1... | collective-permute-start | bytes 884744 | tf_op jit(solution)/shard_map/ppermute | solution.py:153
  55.1 14.4 %collective-permute-start.5 = (bf16[128,1152]{1,0:T(8,128)(2,1)S(1)}, bf16[128,1152]{1,0:T(8,128)(2,1)S(1)}, u32[]{:S(2)}, u32[]{:S(2)}) collective-permute-start(bf16[128,1152]{1,0:T(8,128)(2,1)S(1)} %copy-done.7), channel_id=1, source_target_pairs={{0,192},{64,0},{128,64},{192,128},{1,193},{65,1},{129,65},{193,129... | collective-permute-start | bytes 884744 | tf_op jit(solution)/shard_map/ppermute | solution.py:153
  57.3 13.7 %collective-permute-start.3 = (bf16[128,1152]{1,0:T(8,128)(2,1)S(1)}, bf16[128,1152]{1,0:T(8,128)(2,1)S(1)}, u32[]{:S(2)}, u32[]{:S(2)}) collective-permute-start(bf16[128,1152]{1,0:T(8,128)(2,1)S(1)} %copy-done.7), channel_id=1, source_target_pairs={{0,64},{64,128},{128,192},{192,0},{1,65},{65,129},{129,193},{193,1... | collective-permute-start | bytes 884744 | tf_op jit(solution)/shard_map/ppermute | solution.py:153
  63.1 8.5 %copy-start.3 = (bf16[128,1152]{1,0:T(8,128)(2,1)}, bf16[128,1152]{1,0:T(8,128)(2,1)S(1)}, u32[]{:S(2)}) copy-start(bf16[128,1152]{1,0:T(8,128)(2,1)S(1)} %collective-permute-done.9.refs_5_) | copy-start | bytes 884740
  63.2 11.2 %collective-permute-start.10 = (bf16[64,1152]{1,0:T(8,128)(2,1)S(1)}, bf16[64,1152]{1,0:T(8,128)(2,1)S(1)}, u32[]{:S(2)}, u32[]{:S(2)}) collective-permute-start(bf16[64,1152]{1,0:T(8,128)(2,1)S(1)} %slice.23), channel_id=1, source_target_pairs={{0,192},{64,0},{128,64},{192,128},{1,193},{65,1},{129,65},{193,129... | collective-permute-start | bytes 442376 | tf_op jit(solution)/shard_map/ppermute | solution.py:153
  65.5 6.2 %copy-start.4 = (bf16[128,1152]{1,0:T(8,128)(2,1)}, bf16[128,1152]{1,0:T(8,128)(2,1)S(1)}, u32[]{:S(2)}) copy-start(bf16[128,1152]{1,0:T(8,128)(2,1)S(1)} %collective-permute-done.7.refs_4_) | copy-start | bytes 884740
  65.5 8.9 %collective-permute-start.8 = (bf16[64,1152]{1,0:T(8,128)(2,1)S(1)}, bf16[64,1152]{1,0:T(8,128)(2,1)S(1)}, u32[]{:S(2)}, u32[]{:S(2)}) collective-permute-start(bf16[64,1152]{1,0:T(8,128)(2,1)S(1)} %slice.22), channel_id=1, source_target_pairs={{0,64},{64,128},{128,192},{192,0},{1,65},{65,129},{129,193},{193,1... | collective-permute-start | bytes 442376 | tf_op jit(solution)/shard_map/ppermute | solution.py:153
  69.5 2.2 %copy-start.5 = (bf16[128,1152]{1,0:T(8,128)(2,1)}, bf16[128,1152]{1,0:T(8,128)(2,1)S(1)}, u32[]{:S(2)}) copy-start(bf16[128,1152]{1,0:T(8,128)(2,1)S(1)} %collective-permute-done.5.refs_2_) | copy-start | bytes 884740
  69.5 5.2 %collective-permute-start.6 = (bf16[64,1152]{1,0:T(8,128)(2,1)S(1)}, bf16[64,1152]{1,0:T(8,128)(2,1)S(1)}, u32[]{:S(2)}, u32[]{:S(2)}) collective-permute-start(bf16[64,1152]{1,0:T(8,128)(2,1)S(1)} %slice.21), channel_id=1, source_target_pairs={{0,192},{64,0},{128,64},{192,128},{1,193},{65,1},{129,65},{193,129... | collective-permute-start | bytes 442376 | tf_op jit(solution)/shard_map/ppermute | solution.py:153
  71.0 0.7 copy-start.6
  71.0 6.4 %collective-permute-start.4 = (bf16[64,1152]{1,0:T(8,128)(2,1)S(1)}, bf16[64,1152]{1,0:T(8,128)(2,1)S(1)}, u32[]{:S(2)}, u32[]{:S(2)}) collective-permute-start(bf16[64,1152]{1,0:T(8,128)(2,1)S(1)} %slice.20), channel_id=1, source_target_pairs={{0,64},{64,128},{128,192},{192,0},{1,65},{65,129},{129,193},{193,1... | collective-permute-start | bytes 442376 | tf_op jit(solution)/shard_map/ppermute | solution.py:153
  74.4 3.0 %copy-start.8 = (bf16[64,1152]{1,0:T(8,128)(2,1)}, bf16[64,1152]{1,0:T(8,128)(2,1)S(1)}, u32[]{:S(2)}) copy-start(bf16[64,1152]{1,0:T(8,128)(2,1)S(1)} %collective-permute-done.10.refs_3_) | copy-start | bytes 442372
  74.4 3.0 %copy-start.9 = (bf16[64,1152]{1,0:T(8,128)(2,1)}, bf16[64,1152]{1,0:T(8,128)(2,1)S(1)}, u32[]{:S(2)}) copy-start(bf16[64,1152]{1,0:T(8,128)(2,1)S(1)} %collective-permute-done.8.refs_2_) | copy-start | bytes 442372
  74.7 2.7 %copy-start.10 = (bf16[64,1152]{1,0:T(8,128)(2,1)}, bf16[64,1152]{1,0:T(8,128)(2,1)S(1)}, u32[]{:S(2)}) copy-start(bf16[64,1152]{1,0:T(8,128)(2,1)S(1)} %collective-permute-done.6.refs_1_) | copy-start | bytes 442372
  77.4 0.7 copy-start.11

commit v2 on v0

v2 whole, which is shorter than its diff:
```python
import functools

import jax
import jax.numpy as jnp
from jax import lax
from jax.experimental import pallas as pl
from jax.experimental.pallas import tpu as pltpu
from jax.sharding import Mesh
from jax.sharding import PartitionSpec as P


Q_ROWS = 4096
KV_ROWS = 2048
FSDP = ("y_hi", "y_lo", "z", "core")
AXES = ("rep", *FSDP)
SIZES = (4, 2, 2, 8, 2)
REP = 4

clip_share = 0.5
peak_eps = 1e-06
outer_rate = 0.7
momentum_decay = 0.9

VMEM = pltpu.VMEM
SMALL = pltpu.CompilerParams(vmem_limit_bytes=4 * 1024 * 1024)
WHOLE = pl.BlockSpec(memory_space=pltpu.VMEM)
HBM = pl.BlockSpec(memory_space=pl.ANY)


def far(array):
    return pltpu.with_memory_space_constraint(array, pltpu.HBM)


def near(*arrays):
    return tuple(pltpu.with_memory_space_constraint(a, pltpu.VMEM) for a in arrays)


def columns(me, back, owned):
    return pl.ds(pl.multiple_of(lax.rem(me + back, REP) * owned, 128), owned)


def cut_kernel(aheads, me_ref, local_ref, *refs):
    outs, sems = refs[:-1], refs[-1]
    owned = outs[0].shape[-1]
    copies = []
    for k, (out, (layer, count, ahead)) in enumerate(zip(outs, aheads, strict=True)):
        src = local_ref.at[pl.ds(layer, count), :, columns(me_ref[0], ahead, owned)]
        copies.append(pltpu.make_async_copy(src, out, sems.at[k]))
    for copy in copies:
        copy.start()
    for copy in copies:
        copy.wait()


def cut(local, me, owned, aheads):
    pieces = [VMEM((n, local.shape[1], owned), local.dtype) for _, n, _ in aheads]
    return pl.pallas_call(
        functools.partial(cut_kernel, aheads),
        in_specs=[pl.BlockSpec(memory_space=pltpu.SMEM), HBM],
        out_specs=[WHOLE] * len(aheads),
        out_shape=pieces,
        scratch_shapes=[pltpu.SemaphoreType.DMA((len(aheads),))],
        compiler_params=SMALL,
        name="cut",
    )(me, far(local))


def stage_kernel(me_ref, local_ref, params_ref, moment_ref, own_ref, piece_ref, held_ref, sems):
    mine = columns(me_ref[0], 0, piece_ref.shape[-1])
    copies = (
        pltpu.make_async_copy(local_ref.at[:, :, mine], own_ref, sems.at[0]),
        pltpu.make_async_copy(params_ref.at[:, :, mine], piece_ref, sems.at[1]),
        pltpu.make_async_copy(moment_ref, held_ref, sems.at[2]),
    )
    for copy in copies:
        copy.start()
    for copy in copies:
        copy.wait()


def stage(me, local, params, momentum):
    shape = momentum.shape
    return pl.pallas_call(
        stage_kernel,
        in_specs=[pl.BlockSpec(memory_space=pltpu.SMEM), HBM, HBM, HBM],
        out_specs=[WHOLE, WHOLE, WHOLE],
        out_shape=[VMEM(shape, local.dtype), VMEM(shape, params.dtype), VMEM(shape, jnp.float32)],
        scratch_shapes=[pltpu.SemaphoreType.DMA((3,))],
        compiler_params=SMALL,
        name="stage",
    )(me, far(local), far(params), far(momentum))


def top_kernel(local_ref, out_ref):
    tops = []
    for layer in range(local_ref.shape[0]):
        size = jnp.max(jnp.abs(local_ref[layer]).reshape(8, 16, -1), axis=0)
        tops.append(jnp.max(size.astype(jnp.float32), axis=(0, 1), keepdims=True))
    lane = lax.broadcasted_iota(jnp.int32, out_ref.shape, 1)
    out_ref[...] = jnp.where(lane < out_ref.shape[1] // 2, tops[0], tops[1])


def top_of(local):
    return pl.pallas_call(
        top_kernel,
        in_specs=[WHOLE],
        out_specs=WHOLE,
        out_shape=VMEM((1, 128), jnp.float32),
        compiler_params=SMALL,
        name="top",
    )(*near(local))


def update_kernel(layer, *refs):
    like_ref, top_ref, own_ref, r2_ref, r1_ref, r3_ref, piece_ref, moment_ref, fresh_ref, new_ref = refs
    mates = top_ref.shape[0] // like_ref.shape[0]
    seen = None
    for y in range(like_ref.shape[0]):
        top = jnp.max(top_ref[pl.ds(y * mates, mates)], axis=0)
        top = jnp.where(like_ref[y] == 1, top, 0.0)
        seen = top if seen is None else jnp.maximum(seen, top)
    lane = lax.broadcasted_iota(jnp.int32, seen.shape, 1)
    seen = jnp.where(lane // (seen.shape[1] // 2) == layer, seen, 0.0)
    peak = jnp.max(seen, axis=(0, 1), keepdims=True)
    tau = clip_share * (peak + peak_eps)
    inverse = 1.0 / tau
    quarter = tau * (1.0 / REP)
    _, owned = fresh_ref.shape
    for start in range(0, owned, 128):
        cols = pl.ds(start, 128)
        total = None
        for ref in (own_ref, r1_ref, r2_ref, r3_ref):
            at = min(layer, ref.shape[0] - 1)
            code = jnp.clip(ref[at, :, cols].astype(jnp.float32) * inverse, -1.0, 1.0)
            code = code.astype(jnp.bfloat16).astype(jnp.float32)
            total = code if total is None else total + code
        outer = quarter * total
        fresh_moment = momentum_decay * moment_ref[layer, :, cols] + outer
        fresh = piece_ref[layer, :, cols].astype(jnp.float32)
        fresh = fresh - outer_rate * (outer + momentum_decay * fresh_moment)
        fresh_ref[:, cols] = fresh.astype(jnp.bfloat16)
        new_ref[:, cols] = fresh_moment


def update(layer, like, tops, blocks, piece, moment):
    rows, owned = moment.shape[1:]
    operands = near(tops, *blocks, piece, moment)
    return pl.pallas_call(
        functools.partial(update_kernel, layer),
        in_specs=[pl.BlockSpec(memory_space=pltpu.SMEM)] + [WHOLE] * len(operands),
        out_specs=[WHOLE, WHOLE],
        out_shape=[VMEM((rows, owned), jnp.bfloat16), VMEM((rows, owned), jnp.float32)],
        compiler_params=SMALL,
    )(like, *operands)


def place_kernel(moves, count, me_ref, *refs):
    sems, outs = refs[-1], refs[-1 - count : -1]
    copies = []
    for k, (which, layer, back, first, height) in enumerate(moves):
        src = refs[k]
        owned = src.shape[-1]
        here = columns(me_ref[0], back, owned) if which == 0 else pl.ds(0, owned)
        dst = outs[which].at[layer, pl.ds(first, height), here]
        copies.append(pltpu.make_async_copy(src, dst, sems.at[k]))
    for copy in copies:
        copy.start()
    for copy in copies:
        copy.wait()


def place(me, moves, pieces, shapes, earlier):
    operands = list(near(*pieces))
    aliases = {}
    if earlier is not None:
        aliases = {1 + len(operands) + k: k for k in range(len(earlier))}
        operands += earlier
    return pl.pallas_call(
        functools.partial(place_kernel, moves, len(shapes)),
        in_specs=[pl.BlockSpec(memory_space=pltpu.SMEM)]
        + [WHOLE] * len(pieces)
        + [HBM] * len(aliases),
        out_specs=[HBM] * len(shapes),
        out_shape=shapes,
        scratch_shapes=[pltpu.SemaphoreType.DMA((len(moves),))],
        input_output_aliases=aliases,
        compiler_params=SMALL,
        name="place",
    )(me, *operands)


def shift(value, by):
    return lax.ppermute(value, "rep", [(i, (i + by) % REP) for i in range(REP)])


def tensor_of(y, rows):
    first = y * SIZES[3] * SIZES[4] * rows
    return (first >= Q_ROWS).astype(jnp.int32) + (first >= Q_ROWS + KV_ROWS).astype(jnp.int32)


def on_device(params, deltas, momentum):
    local = deltas[0]
    _, rows, owned = momentum.shape
    me = lax.axis_index("rep").reshape(1)
    b01, b03, b2 = cut(local, me, owned, ((0, 1, 1), (0, 1, 3), (0, 2, 2)))
    top = top_of(local)
    tops = [top, *(shift(top, d) for d in (1, 3, 2))]
    r01, r03 = shift(b01, 1), shift(b03, 3)
    r2 = shift(b2, 2)
    b11, b13 = cut(local, me, owned, ((1, 1, 1), (1, 1, 3)))
    r11, r13 = shift(b11, 1), shift(b13, 3)
    received = [(r2, r01, r03), (r2, r11, r13)]
    y_hi = lax.axis_index("y_hi") * 2
    like = tensor_of(y_hi + lax.iota(jnp.int32, 2), rows) == tensor_of(y_hi + lax.axis_index("y_lo"), rows)
    like = like.astype(jnp.int32)
    top = functools.reduce(jnp.maximum, tops)
    top = jnp.broadcast_to(top[None], (32, 1, 128))
    tops = lax.all_to_all(top, ("y_lo", "z", "core"), 0, 0, tiled=True)
    own, piece, moment = stage(me, local, params, momentum)
    fresh0, new0 = update(0, like, tops, (own, *received[0]), piece, moment)
    right0, left0 = shift(fresh0, 1), shift(fresh0, 3)
    fresh1, new1 = update(1, like, tops, (own, *received[1]), piece, moment)
    right1, left1 = shift(fresh1, 1), shift(fresh1, 3)
    half = rows // 2
    farr0, farl0 = shift(right0[:half], 1), shift(left0[half:], 3)
    farr1, farl1 = shift(right1[:half], 1), shift(left1[half:], 3)
    shapes = [
        jax.ShapeDtypeStruct(params.shape, params.dtype),
        jax.ShapeDtypeStruct(momentum.shape, momentum.dtype),
    ]
    moves = [(0, l, b, 0, rows) for l in range(2) for b in (0, 3, 1)]
    moves += [(1, 0, 0, 0, rows), (1, 1, 0, 0, rows)]
    pieces = (fresh0, right0, left0, fresh1, right1, left1, new0, new1)
    out, new_m = place(me, moves, pieces, shapes, None)
    moves = [(0, l, 2, f, half) for l in range(2) for f in (0, half)]
    (out,) = place(me, moves, (farr0, farl0, farr1, farl1), shapes[:1], (out,))
    return out, new_m


def solution(mesh):
    torus = Mesh(mesh.devices.reshape(SIZES), AXES)
    placed = (P(None, FSDP, None), P("rep", None, FSDP, None), P(None, FSDP, "rep"))
    return jax.shard_map(
        on_device,
        mesh=torus,
        in_specs=placed,
        out_specs=(P(None, FSDP, None), P(None, FSDP, "rep")),
        check_vma=False,
    )
```

time: 131 us -> 71.9 us (0.55)
  the two profiles are of different devices: /device:TPU:1 before, /device:TPU:6 now
where the time goes in v2:
time: 71.9 us; the launch traced here: 71.6 us
  starting transfers between devices  33.7 us (47%)
  waiting for transfers between devices  23.1 us (32%)
  Pallas kernels  12.1 us (17%)
  local copies, waits for them, and re-layouts  1.38 us (2%)
  between operations  0.79 us (1%)
    ppermute x16, starting transfers between devices, shift(): return lax.ppermute(value, 'rep', [(i, (i + by) % REP) for i in range(REP)])  25.1 us
    ppermute x16, waiting for transfers between devices, shift(): return lax.ppermute(value, 'rep', [(i, (i + by) % REP) for i in range(REP)])  16.9 us
    all_to_all x1, starting transfers between devices, on_device(): tops = lax.all_to_all(top, ('y_lo', 'z', 'core'), 0, 0, tiled=True)  8.59 us
    all_to_all x1, waiting for transfers between devices, on_device(): tops = lax.all_to_all(top, ('y_lo', 'z', 'core'), 0, 0, tiled=True)  6.16 us
    pallas_call x2, Pallas kernels, cut(): pl.pallas_call(functools.partial(cut_kernel, aheads), in_specs=[pl.BlockS...  4.32 us
    pallas_call x2, Pallas kernels, update(): pl.pallas_call(functools.partial(update_kernel, layer), in_specs=[pl.Bloc...  3.36 us
    pallas_call x2, Pallas kernels, place(): pl.pallas_call(functools.partial(place_kernel, moves, len(shapes)), in_sp...  2.51 us
    pallas_call x1, Pallas kernels, stage(): pl.pallas_call(stage_kernel, in_specs=[pl.BlockSpec(memory_space=pltpu.SM...  1.66 us
  transfers between devices with their start and end apart: 17, of which 6 were waited for; matrix products, arithmetic and copies ran while one was open for 2% of the time, Pallas kernels for 12%

profile of v2, /device:TPU:6, one launch (start us, length us, event | category | flops | bytes accessed | tf_op | source)
XLA Modules:
  0.0 71.6 jit_solution(18122543921802688979)
XLA Ops:
  0.6 0.0 copy-start
  0.6 2.4 %cut.2 = (bf16[1,128,1152]{2,1,0:T(8,128)(2,1)}, bf16[1,128,1152]{2,1,0:T(8,128)(2,1)}, bf16[2,128,1152]{2,1,0:T(8,128)(2,1)}) custom-call(s32[1]{0:T(128)} %bitcast.me_ref, bf16[2,128,4608]{2,1,0:T(8,128)(2,1)} %bitcast.4), custom_call_target="tpu_custom_call" | custom-call | tf_op jit(solution)/shard_map/cut/pallas_call | solution.py:57
  3.1 1.5 %collective-permute-start.3 = (bf16[2,128,1152]{2,1,0:T(8,128)(2,1)}, bf16[2,128,1152]{2,1,0:T(8,128)(2,1)S(1)}, u32[]{:S(2)}, u32[]{:S(2)}) collective-permute-start(bf16[2,128,1152]{2,1,0:T(8,128)(2,1)} %get-tuple-element.17), channel_id=1, source_target_pairs={{0,128},{64,192},{128,0},{192,64},{1,129},{65,193},{129,1},{193,65... | collective-permute-start | bytes 1769480 | tf_op jit(solution)/shard_map/ppermute | solution.py:193
  4.6 0.0 copy-done
  4.6 0.2 top.1
  4.8 2.2 %collective-permute-start = (f32[1,128]{1,0:T(1,128)S(1)}, f32[1,128]{1,0:T(1,128)S(1)}, u32[]{:S(2)}, u32[]{:S(2)}) collective-permute-start(f32[1,128]{1,0:T(1,128)S(1)} %top.1), channel_id=1, source_target_pairs={{0,64},{64,128},{128,192},{192,0},{1,65},{65,129},{129,193},{193,1... | collective-permute-start | bytes 1544 | tf_op jit(solution)/shard_map/ppermute | solution.py:193
  7.0 0.0 collective-permute-start.1
  7.0 2.1 %collective-permute-start.2 = (f32[1,128]{1,0:T(1,128)S(1)}, f32[1,128]{1,0:T(1,128)S(1)}, u32[]{:S(2)}, u32[]{:S(2)}) collective-permute-start(f32[1,128]{1,0:T(1,128)S(1)} %top.1), channel_id=1, source_target_pairs={{0,128},{64,192},{128,0},{192,64},{1,129},{65,193},{129,1},{193,65... | collective-permute-start | bytes 1544 | tf_op jit(solution)/shard_map/ppermute | solution.py:193
  9.0 1.9 %cut.3 = (bf16[1,128,1152]{2,1,0:T(8,128)(2,1)}, bf16[1,128,1152]{2,1,0:T(8,128)(2,1)}) custom-call(s32[1]{0:T(128)} %bitcast.me_ref, bf16[2,128,4608]{2,1,0:T(8,128)(2,1)} %bitcast.5), custom_call_target="tpu_custom_call" | custom-call | tf_op jit(solution)/shard_map/cut/pallas_call | solution.py:57
  10.9 2.3 %collective-permute-start.10 = (bf16[1,128,1152]{2,1,0:T(8,128)(2,1)}, bf16[1,128,1152]{2,1,0:T(8,128)(2,1)S(1)}, u32[]{:S(2)}, u32[]{:S(2)}) collective-permute-start(bf16[1,128,1152]{2,1,0:T(8,128)(2,1)} %get-tuple-element.23), channel_id=1, source_target_pairs={{0,64},{64,128},{128,192},{192,0},{1,65},{65,129},{129,193},{193,1... | collective-permute-start | bytes 884744 | tf_op jit(solution)/shard_map/ppermute | solution.py:193
  13.2 7.4 %collective-permute-done = f32[1,128]{1,0:T(1,128)S(1)} collective-permute-done((f32[1,128]{1,0:T(1,128)S(1)}, f32[1,128]{1,0:T(1,128)S(1)}, u32[]{:S(2)}, u32[]{:S(2)}) %collective-permute-start) | collective-permute-done | bytes 544 | tf_op jit(solution)/shard_map/ppermute | solution.py:193
  20.7 0.0 collective-permute-start.11
  20.7 0.0 collective-permute-done.1
  20.7 3.2 %collective-permute-start.4 = (bf16[1,128,1152]{2,1,0:T(8,128)(2,1)}, bf16[1,128,1152]{2,1,0:T(8,128)(2,1)S(1)}, u32[]{:S(2)}, u32[]{:S(2)}) collective-permute-start(bf16[1,128,1152]{2,1,0:T(8,128)(2,1)} %get-tuple-element.18), channel_id=1, source_target_pairs={{0,64},{64,128},{128,192},{192,0},{1,65},{65,129},{129,193},{193,1... | collective-permute-start | bytes 884744 | tf_op jit(solution)/shard_map/ppermute | solution.py:193
  23.9 0.0 collective-permute-done.2
  23.9 0.0 collective-permute-start.5
  23.9 0.6 broadcast_in_dim.9
  24.5 8.6 %all-to-all-start = ((f32[32,1,128]{2,1,0:T(1,128)}), f32[32,1,128]{2,1,0:T(1,128)S(1)}, u32[]{:S(2)}, u32[]{:S(2)}) async-start(f32[32,1,128]{2,1,0:T(1,128)} %broadcast_in_dim.9), calls=%async_computation | async-start | bytes 32768 | tf_op jit(solution)/shard_map/all_to_all | solution.py:218
  33.1 0.6 compare_convert_fusion.refs_0_
  33.7 1.7 %stage.1 = (bf16[2,128,1152]{2,1,0:T(8,128)(2,1)S(1)}, bf16[2,128,1152]{2,1,0:T(8,128)(2,1)S(1)}, f32[2,128,1152]{2,1,0:T(8,128)S(1)}) custom-call(s32[1]{0:T(128)} %bitcast.me_ref, bf16[2,128,4608]{2,1,0:T(8,128)(2,1)} %bitcast.6, bf16[2,128,4608]{2,1,0:T(8,128)(2,1)} %params_ref.1, f32[2,128,1152]{2,1,0:T(8,128)} %moment_ref.1), custom_call_target="tpu_custom_call" | custom-call | tf_op jit(solution)/shard_map/stage/pallas_call | solution.py:83
  35.4 6.2 %all-to-all-done.refs_1_ = f32[32,1,128]{2,1,0:T(1,128)S(1)} async-done(((f32[32,1,128]{2,1,0:T(1,128)}), f32[32,1,128]{2,1,0:T(1,128)S(1)}, u32[]{:S(2)}, u32[]{:S(2)}) %all-to-all-start) | async-done | bytes 16416 | tf_op jit(solution)/shard_map/all_to_all | solution.py:218
  41.5 0.0 copy-start.2
  41.5 0.0 collective-permute-done.10.refs_4_
  41.5 0.0 collective-permute-done.11.refs_5_
  41.5 0.0 collective-permute-done.3.refs_3_
  41.6 0.0 copy-start.1
  41.6 0.7 copy-done.1
  42.3 1.7 %shard_map.51 = (bf16[128,1152]{1,0:T(8,128)(2,1)S(1)}, f32[128,1152]{1,0:T(8,128)S(1)}) custom-call(s32[2]{0:T(128)S(1)} %copy-done.1, f32[32,1,128]{2,1,0:T(1,128)S(1)} %all-to-all-done.refs_1_, bf16[2,128,1152]{2,1,0:T(8,128)(2,1)S(1)} %get-tuple-element.16.refs_2_, bf16[2,128,1152]{2,1,0:T(8,128)(2,1)S(1)} %collective-permute-done.3.refs_3_, ...), custom_call_target="tpu_custom_call" | custom-call | tf_op jit(solution)/shard_map/pallas_call | solution.py:148
  44.0 2.9 %collective-permute-start.12 = (bf16[128,1152]{1,0:T(8,128)(2,1)S(1)}, bf16[128,1152]{1,0:T(8,128)(2,1)S(1)}, u32[]{:S(2)}, u32[]{:S(2)}) collective-permute-start(bf16[128,1152]{1,0:T(8,128)(2,1)S(1)} %get-tuple-element.25.refs_3_), channel_id=1, source_target_pairs={{0,64},{64,128},{128,192},{192,0},{1,65},{65,129},{129,193},{193,1... | collective-permute-start | bytes 884744 | tf_op jit(solution)/shard_map/ppermute | solution.py:193
  46.9 0.0 collective-permute-start.14
  46.9 0.0 collective-permute-done.4.refs_4_
  46.9 0.0 collective-permute-done.5.refs_5_
  46.9 0.0 copy-done.2
  46.9 1.7 %shard_map.50 = (bf16[128,1152]{1,0:T(8,128)(2,1)S(1)}, f32[128,1152]{1,0:T(8,128)S(1)}) custom-call(s32[2]{0:T(128)S(1)} %copy-done.2, f32[32,1,128]{2,1,0:T(1,128)S(1)} %all-to-all-done.refs_1_, bf16[2,128,1152]{2,1,0:T(8,128)(2,1)S(1)} %get-tuple-element.16.refs_2_, bf16[2,128,1152]{2,1,0:T(8,128)(2,1)S(1)} %collective-permute-done.3.refs_3_, ...), custom_call_target="tpu_custom_call" | custom-call | tf_op jit(solution)/shard_map/pallas_call | solution.py:148
  48.6 3.3 %collective-permute-start.6 = (bf16[128,1152]{1,0:T(8,128)(2,1)S(1)}, bf16[128,1152]{1,0:T(8,128)(2,1)S(1)}, u32[]{:S(2)}, u32[]{:S(2)}) collective-permute-start(bf16[128,1152]{1,0:T(8,128)(2,1)S(1)} %get-tuple-element.22.refs_0_), channel_id=1, source_target_pairs={{0,64},{64,128},{128,192},{192,0},{1,65},{65,129},{129,193},{193,1... | collective-permute-start | bytes 884744 | tf_op jit(solution)/shard_map/ppermute | solution.py:193
  51.9 0.0 collective-permute-start.8
  51.9 2.4 %collective-permute-done.12.refs_4_ = bf16[128,1152]{1,0:T(8,128)(2,1)S(1)} collective-permute-done((bf16[128,1152]{1,0:T(8,128)(2,1)S(1)}, bf16[128,1152]{1,0:T(8,128)(2,1)S(1)}, u32[]{:S(2)}, u32[]{:S(2)}) %collective-permute-start.12) | collective-permute-done | bytes 294944 | tf_op jit(solution)/shard_map/ppermute | solution.py:193
  54.3 3.8 %collective-permute-start.13 = (bf16[64,1152]{1,0:T(8,128)(2,1)S(1)}, bf16[64,1152]{1,0:T(8,128)(2,1)S(1)}, u32[]{:S(2)}, u32[]{:S(2)}) collective-permute-start(bf16[64,1152]{1,0:T(8,128)(2,1)S(1)} %slice.18), channel_id=1, source_target_pairs={{0,64},{64,128},{128,192},{192,0},{1,65},{65,129},{129,193},{193,1... | collective-permute-start | bytes 442376 | tf_op jit(solution)/shard_map/ppermute | solution.py:193
  58.0 0.0 collective-permute-done.14.refs_5_
  58.1 0.1 collective-permute-start.15
  58.1 2.4 %collective-permute-done.6.refs_1_ = bf16[128,1152]{1,0:T(8,128)(2,1)S(1)} collective-permute-done((bf16[128,1152]{1,0:T(8,128)(2,1)S(1)}, bf16[128,1152]{1,0:T(8,128)(2,1)S(1)}, u32[]{:S(2)}, u32[]{:S(2)}) %collective-permute-start.6) | collective-permute-done | bytes 294944 | tf_op jit(solution)/shard_map/ppermute | solution.py:193
  60.6 3.8 %collective-permute-start.7 = (bf16[64,1152]{1,0:T(8,128)(2,1)S(1)}, bf16[64,1152]{1,0:T(8,128)(2,1)S(1)}, u32[]{:S(2)}, u32[]{:S(2)}) collective-permute-start(bf16[64,1152]{1,0:T(8,128)(2,1)S(1)} %slice.16), channel_id=1, source_target_pairs={{0,64},{64,128},{128,192},{192,0},{1,65},{65,129},{129,193},{193,1... | collective-permute-start | bytes 442376 | tf_op jit(solution)/shard_map/ppermute | solution.py:193
  64.4 0.0 collective-permute-done.8.refs_2_
  64.4 0.1 collective-permute-start.9
  64.5 1.7 %place.2 = (bf16[2,128,4608]{2,1,0:T(8,128)(2,1)}, f32[2,128,1152]{2,1,0:T(8,128)}) custom-call(s32[1]{0:T(128)} %bitcast.me_ref, bf16[128,1152]{1,0:T(8,128)(2,1)S(1)} %get-tuple-element.22.refs_0_, bf16[128,1152]{1,0:T(8,128)(2,1)S(1)} %collective-permute-done.6.refs_1_, bf16[128,1152]{1,0:T(8,128)(2,1)S(1)} %collective-permute-done.8.refs_2_, ...), custom_call_target="tpu_custom_call" | custom-call | tf_op jit(solution)/shard_map/place/pallas_call | solution.py:178
  66.1 0.0 collective-permute-done.13.refs_2_
  66.2 0.0 collective-permute-done.15.refs_3_
  66.2 0.8 %collective-permute-done.7.refs_0_ = bf16[64,1152]{1,0:T(8,128)(2,1)S(1)} collective-permute-done((bf16[64,1152]{1,0:T(8,128)(2,1)S(1)}, bf16[64,1152]{1,0:T(8,128)(2,1)S(1)}, u32[]{:S(2)}, u32[]{:S(2)}) %collective-permute-start.7) | collective-permute-done | bytes 147488 | tf_op jit(solution)/shard_map/ppermute | solution.py:193
  67.0 3.8 %collective-permute-done.9.refs_1_ = bf16[64,1152]{1,0:T(8,128)(2,1)S(1)} collective-permute-done((bf16[64,1152]{1,0:T(8,128)(2,1)S(1)}, bf16[64,1152]{1,0:T(8,128)(2,1)S(1)}, u32[]{:S(2)}, u32[]{:S(2)}) %collective-permute-start.9) | collective-permute-done | bytes 147488 | tf_op jit(solution)/shard_map/ppermute | solution.py:193
  70.8 0.8 %place.3 = bf16[2,128,4608]{2,1,0:T(8,128)(2,1)} custom-call(s32[1]{0:T(128)} %bitcast.me_ref, bf16[64,1152]{1,0:T(8,128)(2,1)S(1)} %collective-permute-done.7.refs_0_, bf16[64,1152]{1,0:T(8,128)(2,1)S(1)} %collective-permute-done.9.refs_1_, bf16[64,1152]{1,0:T(8,128)(2,1)S(1)} %collective-permute-done.13.refs_2_, ...), custom_call_target="tpu_custom_call", output_to_operand_aliasing={{}: (5, {})} | custom-call | tf_op jit(solution)/shard_map/place/pallas_call | solution.py:178
  (5 shorter events, 0.1 us)
Async XLA Ops:
  0.6 4.0 %copy-start = (bf16[1,2,128,4608]{3,2,1,0:T(8,128)(2,1)S(1)}, bf16[1,2,128,4608]{3,2,1,0:T(8,128)(2,1)}, u32[]{:S(2)}) copy-start(bf16[1,2,128,4608]{3,2,1,0:T(8,128)(2,1)} %param.4) | copy-start | bytes 7077892
  3.1 38.5 %collective-permute-start.3 = (bf16[2,128,1152]{2,1,0:T(8,128)(2,1)}, bf16[2,128,1152]{2,1,0:T(8,128)(2,1)S(1)}, u32[]{:S(2)}, u32[]{:S(2)}) collective-permute-start(bf16[2,128,1152]{2,1,0:T(8,128)(2,1)} %get-tuple-element.17), channel_id=1, source_target_pairs={{0,128},{64,192},{128,0},{192,64},{1,129},{65,193},{129,1},{193,65... | collective-permute-start | bytes 1769480 | tf_op jit(solution)/shard_map/ppermute | solution.py:193
  4.8 15.8 %collective-permute-start = (f32[1,128]{1,0:T(1,128)S(1)}, f32[1,128]{1,0:T(1,128)S(1)}, u32[]{:S(2)}, u32[]{:S(2)}) collective-permute-start(f32[1,128]{1,0:T(1,128)S(1)} %top.1), channel_id=1, source_target_pairs={{0,64},{64,128},{128,192},{192,0},{1,65},{65,129},{129,193},{193,1... | collective-permute-start | bytes 1544 | tf_op jit(solution)/shard_map/ppermute | solution.py:193
  7.0 13.7 %collective-permute-start.1 = (f32[1,128]{1,0:T(1,128)S(1)}, f32[1,128]{1,0:T(1,128)S(1)}, u32[]{:S(2)}, u32[]{:S(2)}) collective-permute-start(f32[1,128]{1,0:T(1,128)S(1)} %top.1), channel_id=1, source_target_pairs={{0,192},{64,0},{128,64},{192,128},{1,193},{65,1},{129,65},{193,129... | collective-permute-start | bytes 1544 | tf_op jit(solution)/shard_map/ppermute | solution.py:193
  7.0 16.9 %collective-permute-start.2 = (f32[1,128]{1,0:T(1,128)S(1)}, f32[1,128]{1,0:T(1,128)S(1)}, u32[]{:S(2)}, u32[]{:S(2)}) collective-permute-start(f32[1,128]{1,0:T(1,128)S(1)} %top.1), channel_id=1, source_target_pairs={{0,128},{64,192},{128,0},{192,64},{1,129},{65,193},{129,1},{193,65... | collective-permute-start | bytes 1544 | tf_op jit(solution)/shard_map/ppermute | solution.py:193
  10.9 30.6 %collective-permute-start.10 = (bf16[1,128,1152]{2,1,0:T(8,128)(2,1)}, bf16[1,128,1152]{2,1,0:T(8,128)(2,1)S(1)}, u32[]{:S(2)}, u32[]{:S(2)}) collective-permute-start(bf16[1,128,1152]{2,1,0:T(8,128)(2,1)} %get-tuple-element.23), channel_id=1, source_target_pairs={{0,64},{64,128},{128,192},{192,0},{1,65},{65,129},{129,193},{193,1... | collective-permute-start | bytes 884744 | tf_op jit(solution)/shard_map/ppermute | solution.py:193
  20.7 20.9 %collective-permute-start.11 = (bf16[1,128,1152]{2,1,0:T(8,128)(2,1)}, bf16[1,128,1152]{2,1,0:T(8,128)(2,1)}, u32[]{:S(2)}, u32[]{:S(2)}) collective-permute-start(bf16[1,128,1152]{2,1,0:T(8,128)(2,1)} %get-tuple-element.24), channel_id=1, source_target_pairs={{0,192},{64,0},{128,64},{192,128},{1,193},{65,1},{129,65},{193,129... | collective-permute-start | bytes 884744 | tf_op jit(solution)/shard_map/ppermute | solution.py:193
  20.7 26.2 %collective-permute-start.4 = (bf16[1,128,1152]{2,1,0:T(8,128)(2,1)}, bf16[1,128,1152]{2,1,0:T(8,128)(2,1)S(1)}, u32[]{:S(2)}, u32[]{:S(2)}) collective-permute-start(bf16[1,128,1152]{2,1,0:T(8,128)(2,1)} %get-tuple-element.18), channel_id=1, source_target_pairs={{0,64},{64,128},{128,192},{192,0},{1,65},{65,129},{129,193},{193,1... | collective-permute-start | bytes 884744 | tf_op jit(solution)/shard_map/ppermute | solution.py:193
  23.9 23.0 %collective-permute-start.5 = (bf16[1,128,1152]{2,1,0:T(8,128)(2,1)}, bf16[1,128,1152]{2,1,0:T(8,128)(2,1)}, u32[]{:S(2)}, u32[]{:S(2)}) collective-permute-start(bf16[1,128,1152]{2,1,0:T(8,128)(2,1)} %get-tuple-element.19), channel_id=1, source_target_pairs={{0,192},{64,0},{128,64},{192,128},{1,193},{65,1},{129,65},{193,129... | collective-permute-start | bytes 884744 | tf_op jit(solution)/shard_map/ppermute | solution.py:193
  24.5 17.0 %all-to-all-start = ((f32[32,1,128]{2,1,0:T(1,128)}), f32[32,1,128]{2,1,0:T(1,128)S(1)}, u32[]{:S(2)}, u32[]{:S(2)}) async-start(f32[32,1,128]{2,1,0:T(1,128)} %broadcast_in_dim.9), calls=%async_computation | async-start | bytes 32768 | tf_op jit(solution)/shard_map/all_to_all | solution.py:218
  41.5 5.3 %copy-start.2 = (s32[2]{0:T(128)S(1)}, s32[2]{0:T(128)}, u32[]{:S(2)}) copy-start(s32[2]{0:T(128)} %compare_convert_fusion.refs_0_) | copy-start | bytes 28
  41.6 0.7 %copy-start.1 = (s32[2]{0:T(128)S(1)}, s32[2]{0:T(128)}, u32[]{:S(2)}) copy-start(s32[2]{0:T(128)} %compare_convert_fusion.refs_0_) | copy-start | bytes 28
  44.0 10.3 %collective-permute-start.12 = (bf16[128,1152]{1,0:T(8,128)(2,1)S(1)}, bf16[128,1152]{1,0:T(8,128)(2,1)S(1)}, u32[]{:S(2)}, u32[]{:S(2)}) collective-permute-start(bf16[128,1152]{1,0:T(8,128)(2,1)S(1)} %get-tuple-element.25.refs_3_), channel_id=1, source_target_pairs={{0,64},{64,128},{128,192},{192,0},{1,65},{65,129},{129,193},{193,1... | collective-permute-start | bytes 884744 | tf_op jit(solution)/shard_map/ppermute | solution.py:193
  46.9 11.2 %collective-permute-start.14 = (bf16[128,1152]{1,0:T(8,128)(2,1)S(1)}, bf16[128,1152]{1,0:T(8,128)(2,1)S(1)}, u32[]{:S(2)}, u32[]{:S(2)}) collective-permute-start(bf16[128,1152]{1,0:T(8,128)(2,1)S(1)} %get-tuple-element.25.refs_3_), channel_id=1, source_target_pairs={{0,192},{64,0},{128,64},{192,128},{1,193},{65,1},{129,65},{193,129... | collective-permute-start | bytes 884744 | tf_op jit(solution)/shard_map/ppermute | solution.py:193
  48.6 12.0 %collective-permute-start.6 = (bf16[128,1152]{1,0:T(8,128)(2,1)S(1)}, bf16[128,1152]{1,0:T(8,128)(2,1)S(1)}, u32[]{:S(2)}, u32[]{:S(2)}) collective-permute-start(bf16[128,1152]{1,0:T(8,128)(2,1)S(1)} %get-tuple-element.22.refs_0_), channel_id=1, source_target_pairs={{0,64},{64,128},{128,192},{192,0},{1,65},{65,129},{129,193},{193,1... | collective-permute-start | bytes 884744 | tf_op jit(solution)/shard_map/ppermute | solution.py:193
  51.9 12.5 %collective-permute-start.8 = (bf16[128,1152]{1,0:T(8,128)(2,1)S(1)}, bf16[128,1152]{1,0:T(8,128)(2,1)S(1)}, u32[]{:S(2)}, u32[]{:S(2)}) collective-permute-start(bf16[128,1152]{1,0:T(8,128)(2,1)S(1)} %get-tuple-element.22.refs_0_), channel_id=1, source_target_pairs={{0,192},{64,0},{128,64},{192,128},{1,193},{65,1},{129,65},{193,129... | collective-permute-start | bytes 884744 | tf_op jit(solution)/shard_map/ppermute | solution.py:193
  54.3 11.9 %collective-permute-start.13 = (bf16[64,1152]{1,0:T(8,128)(2,1)S(1)}, bf16[64,1152]{1,0:T(8,128)(2,1)S(1)}, u32[]{:S(2)}, u32[]{:S(2)}) collective-permute-start(bf16[64,1152]{1,0:T(8,128)(2,1)S(1)} %slice.18), channel_id=1, source_target_pairs={{0,64},{64,128},{128,192},{192,0},{1,65},{65,129},{129,193},{193,1... | collective-permute-start | bytes 442376 | tf_op jit(solution)/shard_map/ppermute | solution.py:193
  58.1 8.1 %collective-permute-start.15 = (bf16[64,1152]{1,0:T(8,128)(2,1)S(1)}, bf16[64,1152]{1,0:T(8,128)(2,1)S(1)}, u32[]{:S(2)}, u32[]{:S(2)}) collective-permute-start(bf16[64,1152]{1,0:T(8,128)(2,1)S(1)} %slice.19), channel_id=1, source_target_pairs={{0,192},{64,0},{128,64},{192,128},{1,193},{65,1},{129,65},{193,129... | collective-permute-start | bytes 442376 | tf_op jit(solution)/shard_map/ppermute | solution.py:193
  60.6 6.4 %collective-permute-start.7 = (bf16[64,1152]{1,0:T(8,128)(2,1)S(1)}, bf16[64,1152]{1,0:T(8,128)(2,1)S(1)}, u32[]{:S(2)}, u32[]{:S(2)}) collective-permute-start(bf16[64,1152]{1,0:T(8,128)(2,1)S(1)} %slice.16), channel_id=1, source_target_pairs={{0,64},{64,128},{128,192},{192,0},{1,65},{65,129},{129,193},{193,1... | collective-permute-start | bytes 442376 | tf_op jit(solution)/shard_map/ppermute | solution.py:193
  64.4 6.4 %collective-permute-start.9 = (bf16[64,1152]{1,0:T(8,128)(2,1)S(1)}, bf16[64,1152]{1,0:T(8,128)(2,1)S(1)}, u32[]{:S(2)}, u32[]{:S(2)}) collective-permute-start(bf16[64,1152]{1,0:T(8,128)(2,1)S(1)} %slice.17), channel_id=1, source_target_pairs={{0,192},{64,0},{128,64},{192,128},{1,193},{65,1},{129,65},{193,129... | collective-permute-start | bytes 442376 | tf_op jit(solution)/shard_map/ppermute | solution.py:193

commit v3 on v2

v3 whole, which is shorter than its diff:
```python
import functools

import jax
import jax.numpy as jnp
from jax import lax
from jax.experimental import pallas as pl
from jax.experimental.pallas import tpu as pltpu
from jax.sharding import Mesh
from jax.sharding import PartitionSpec as P


Q_ROWS = 4096
KV_ROWS = 2048
FSDP = ("y_hi", "y_lo", "z", "core")
AXES = ("rep", *FSDP)
SIZES = (4, 2, 2, 8, 2)
REP = 4

clip_share = 0.5
peak_eps = 1e-06
outer_rate = 0.7
momentum_decay = 0.9

VMEM = pltpu.VMEM
SMALL = pltpu.CompilerParams(vmem_limit_bytes=4 * 1024 * 1024)
WHOLE = pl.BlockSpec(memory_space=pltpu.VMEM)
SCALARS = pl.BlockSpec(memory_space=pltpu.SMEM)
HBM = pl.BlockSpec(memory_space=pl.ANY)


def far(array):
    return pltpu.with_memory_space_constraint(array, pltpu.HBM)


def near(*arrays):
    return tuple(pltpu.with_memory_space_constraint(a, pltpu.VMEM) for a in arrays)


def columns(ahead, owned):
    return pl.ds(pl.multiple_of(lax.rem(lax.axis_index("rep") + ahead, REP) * owned, 128), owned)


def run_all(copies):
    for copy in copies:
        copy.start()
    for copy in copies:
        copy.wait()


def open_kernel(moves, local_ref, *refs):
    outs, (top_ref, held_ref, sems) = refs[:-3], refs[-3:]
    layers, rows, width = local_ref.shape
    owned = width // REP
    count = sems.shape[0] // layers
    step = rows // count
    loads = []
    for layer in range(layers):
        for k in range(count):
            here = (layer, pl.ds(k * step, step))
            sem = sems.at[layer * count + k]
            loads.append(pltpu.make_async_copy(local_ref.at[here], held_ref.at[here], sem))
    for load in loads:
        load.start()
    tops = []
    for layer in range(layers):
        size = None
        for k in range(count):
            loads[layer * count + k].wait()
            here = slice(k * step, (k + 1) * step)
            for which, at, first, last, ahead in moves[layer]:
                if first <= k * step < last:
                    block = held_ref[layer, here, columns(ahead, owned)]
                    outs[which][(*at, here)] = block
            chunk = jnp.max(jnp.abs(held_ref[layer, here]).reshape(step // 16, 16, width), axis=0)
            size = chunk if size is None else jnp.maximum(size, chunk)
        tops.append(jnp.max(size.astype(jnp.float32), axis=(0, 1), keepdims=True))
    lane = lax.broadcasted_iota(jnp.int32, top_ref.shape, 1)
    top_ref[...] = jnp.where(lane < top_ref.shape[1] // 2, tops[0], tops[1])


def open_up(local, moves, shapes):
    outs = [VMEM(shape, local.dtype) for shape in shapes]
    outs += [VMEM((1, 128), jnp.float32)]
    return pl.pallas_call(
        functools.partial(open_kernel, moves),
        in_specs=[HBM],
        out_specs=[WHOLE] * len(outs),
        out_shape=outs,
        scratch_shapes=[VMEM(local.shape, local.dtype), pltpu.SemaphoreType.DMA((8,))],
        compiler_params=pltpu.CompilerParams(vmem_limit_bytes=8 * 1024 * 1024),
        name="open",
    )(far(local))


def load_kernel(moves, *refs):
    count = len(moves)
    sources, outs, sems = refs[: -count - 1], refs[-count - 1 : -1], refs[-1]
    owned = outs[0].shape[-1]
    copies = []
    for k, (which, at, ahead) in enumerate(moves):
        src = sources[which].at[at]
        if ahead is not None:
            src = sources[which].at[at, :, columns(ahead, owned)]
        copies.append(pltpu.make_async_copy(src, outs[k], sems.at[k]))
    run_all(copies)


def load(sources, moves, shapes):
    return pl.pallas_call(
        functools.partial(load_kernel, moves),
        in_specs=[HBM] * len(sources),
        out_specs=[WHOLE] * len(moves),
        out_shape=[VMEM(s, sources[m[0]].dtype) for s, m in zip(shapes, moves, strict=True)],
        scratch_shapes=[pltpu.SemaphoreType.DMA((len(moves),))],
        compiler_params=SMALL,
        name="load",
    )(*map(far, sources))


def meet_kernel(*refs):
    top = functools.reduce(jnp.maximum, [ref[...] for ref in refs[:-1]])
    refs[-1][...] = jnp.broadcast_to(top[None], refs[-1].shape)


def meet(tops, count):
    return pl.pallas_call(
        meet_kernel,
        in_specs=[WHOLE] * len(tops),
        out_specs=WHOLE,
        out_shape=VMEM((count, 1, 128), jnp.float32),
        compiler_params=SMALL,
        name="meet",
    )(*near(*tops))


def tau_of(like_ref, top_ref, layer):
    mates = top_ref.shape[0] // like_ref.shape[0]
    seen = None
    for y in range(like_ref.shape[0]):
        top = jnp.max(top_ref[pl.ds(y * mates, mates)], axis=0)
        top = jnp.where(like_ref[y] == 1, top, 0.0)
        seen = top if seen is None else jnp.maximum(seen, top)
    lane = lax.broadcasted_iota(jnp.int32, seen.shape, 1)
    seen = jnp.where(lane // (seen.shape[1] // 2) == layer, seen, 0.0)
    return clip_share * (jnp.max(seen, axis=(0, 1), keepdims=True) + peak_eps)


def code_of(block, inverse):
    code = jnp.clip(block.astype(jnp.float32) * inverse, -1.0, 1.0)
    return code.astype(jnp.bfloat16).astype(jnp.float32)


def update_kernel(layer, like_ref, top_ref, *refs):
    blocks, (piece_ref, moment_ref, fresh_ref, new_ref) = refs[:-4], refs[-4:]
    tau = tau_of(like_ref, top_ref, layer)
    inverse = 1.0 / tau
    quarter = tau * (1.0 / REP)
    _, owned = fresh_ref.shape
    for start in range(0, owned, 128):
        cols = pl.ds(start, 128)
        raw = [ref[layer, :, cols] if len(ref.shape) == 3 else ref[:, cols] for ref in blocks]
        total = functools.reduce(jnp.add, [code_of(block, inverse) for block in raw])
        outer = quarter * total
        fresh_moment = momentum_decay * moment_ref[:, cols] + outer
        fresh = piece_ref[:, cols].astype(jnp.float32)
        fresh = fresh - outer_rate * (outer + momentum_decay * fresh_moment)
        fresh_ref[:, cols] = fresh.astype(jnp.bfloat16)
        new_ref[:, cols] = fresh_moment


def update(layer, like, tops, blocks, piece, moment):
    rows, owned = moment.shape
    operands = near(tops, *blocks, piece, moment)
    return pl.pallas_call(
        functools.partial(update_kernel, layer),
        in_specs=[SCALARS] + [WHOLE] * len(operands),
        out_specs=[WHOLE, WHOLE],
        out_shape=[VMEM((rows, owned), jnp.bfloat16), VMEM((rows, owned), jnp.float32)],
        compiler_params=SMALL,
    )(like, *operands)


def place_kernel(moves, count, *refs):
    sems, outs = refs[-1], refs[-1 - count : -1]
    copies = []
    for k, (which, layer, back, first, height) in enumerate(moves):
        src = refs[k]
        owned = src.shape[-1]
        here = columns(back, owned) if which == 0 else pl.ds(0, owned)
        dst = outs[which].at[layer, pl.ds(first, height), here]
        copies.append(pltpu.make_async_copy(src, dst, sems.at[k]))
    run_all(copies)


def place(moves, pieces, shapes, earlier):
    operands = list(near(*pieces))
    aliases = {}
    if earlier is not None:
        aliases = {len(operands) + k: k for k in range(len(earlier))}
        operands += earlier
    return pl.pallas_call(
        functools.partial(place_kernel, moves, len(shapes)),
        in_specs=[WHOLE] * len(pieces) + [HBM] * len(aliases),
        out_specs=[HBM] * len(shapes),
        out_shape=shapes,
        scratch_shapes=[pltpu.SemaphoreType.DMA((len(moves),))],
        input_output_aliases=aliases,
        compiler_params=SMALL,
        name="place",
    )(*operands)


def shift(value, by):
    return lax.ppermute(value, "rep", [(i, (i + by) % REP) for i in range(REP)])


def tensor_of(y, rows):
    first = y * SIZES[3] * SIZES[4] * rows
    return (first >= Q_ROWS).astype(jnp.int32) + (first >= Q_ROWS + KV_ROWS).astype(jnp.int32)


def on_device(params, deltas, momentum):
    local = deltas[0]
    _, rows, owned = momentum.shape
    half = rows // 2
    first = ((0, (), 0, rows, 1), (1, (), 0, rows, 3), (2, (0,), 0, rows, 2))
    second = ((2, (1,), 0, rows, 2),)
    flat = (rows, owned)
    b01, b03, b2, top = open_up(local, (first, second), (flat, flat, (2, *flat)))
    tops = [top, *(shift(top, d) for d in (1, 3, 2))]
    r01, r03, r2 = shift(b01, 1), shift(b03, 3), shift(b2, 2)
    b11, b13 = load((local,), ((0, 1, 1), (0, 1, 3)), (flat, flat))
    r11, r13 = shift(b11, 1), shift(b13, 3)
    y_hi = lax.axis_index("y_hi") * 2
    own_tensor = tensor_of(y_hi + lax.axis_index("y_lo"), rows)
    like = tensor_of(y_hi + lax.iota(jnp.int32, 2), rows) == own_tensor
    like = like.astype(jnp.int32)
    top = meet(tops, 32)
    tops = lax.all_to_all(top, ("y_lo", "z", "core"), 0, 0, tiled=True)
    moves = ((0, 0, 0), (1, 0, 0), (2, 0, None))
    staged0 = load((local, params, momentum), moves, [flat] * 3)
    fresh0, new0 = update(0, like, tops, (staged0[0], r01, r2, r03), *staged0[1:])
    right0, left0 = shift(fresh0, 1), shift(fresh0, 3)
    moves = ((0, 1, 0), (1, 1, 0), (2, 1, None))
    staged1 = load((local, params, momentum), moves, [flat] * 3)
    fresh1, new1 = update(1, like, tops, (staged1[0], r11, r2, r13), *staged1[1:])
    right1, left1 = shift(fresh1, 1), shift(fresh1, 3)
    farr0, farl0 = shift(right0[:half], 1), shift(left0[half:], 3)
    farr1, farl1 = shift(right1[:half], 1), shift(left1[half:], 3)
    shapes = [
        jax.ShapeDtypeStruct(params.shape, params.dtype),
        jax.ShapeDtypeStruct(momentum.shape, momentum.dtype),
    ]
    moves = [(0, l, b, 0, rows) for l in range(2) for b in (0, 3, 1)]
    moves += [(0, 0, 2, 0, half), (0, 0, 2, half, half)]
    moves += [(1, 0, 0, 0, rows), (1, 1, 0, 0, rows)]
    pieces = (fresh0, right0, left0, fresh1, right1, left1, farr0, farl0, new0, new1)
    out, new_m = place(moves, pieces, shapes, None)
    moves = [(0, 1, 2, 0, half), (0, 1, 2, half, half)]
    (out,) = place(moves, (farr1, farl1), shapes[:1], (out,))
    return out, new_m


def solution(mesh):
    torus = Mesh(mesh.devices.reshape(SIZES), AXES)
    placed = (P(None, FSDP, None), P("rep", None, FSDP, None), P(None, FSDP, "rep"))
    return jax.shard_map(
        on_device,
        mesh=torus,
        in_specs=placed,
        out_specs=(P(None, FSDP, None), P(None, FSDP, "rep")),
        check_vma=False,
    )
```

time: 71.9 us -> 75.4 us (1.049)
  local copies, waits for them, and re-layouts: 1.38 us -> 4.04 us
    unnamed x6 -> x10, local copies, waits for them, and re-layouts: 0.73 us -> 3.99 us
    ppermute x16, waiting for transfers between devices: 16.9 us -> 19.5 us  [shift(): return lax.ppermute(value, 'rep', [(i, (i + by) % REP) for i in range(REP)])]
    all_to_all x1, waiting for transfers between devices: 6.16 us -> 3.82 us  [on_device(): tops = lax.all_to_all(top, ('y_lo', 'z', 'core'), 0, 0, tiled=True)]
    pallas_call x6 -> x7, Pallas kernels: 9.57 us -> 10.2 us  [the longest x3 4.44 us: load(): pl.pallas_call(functools.partial(load_kernel, moves), in_specs=[HBM] * le...]
  transfers between devices with their start and end apart: 17 -> 17, of which waited for: 6 -> 6; matrix products, arithmetic and copies ran while one was open for 2% -> 1% of each run, Pallas kernels for 12% -> 12%
where the time goes in v3:
time: 75.4 us; the launch traced here: 75.1 us
  starting transfers between devices  33.6 us (45%)
  waiting for transfers between devices  23.4 us (31%)
  Pallas kernels  12.7 us (17%)
  local copies, waits for them, and re-layouts  4.04 us (5%)
  between operations  0.79 us (1%)
    ppermute x16, starting transfers between devices, shift(): return lax.ppermute(value, 'rep', [(i, (i + by) % REP) for i in range(REP)])  25 us
    ppermute x16, waiting for transfers between devices, shift(): return lax.ppermute(value, 'rep', [(i, (i + by) % REP) for i in range(REP)])  19.5 us
    all_to_all x1, starting transfers between devices, on_device(): tops = lax.all_to_all(top, ('y_lo', 'z', 'core'), 0, 0, tiled=True)  8.6 us
    pallas_call x3, Pallas kernels, load(): pl.pallas_call(functools.partial(load_kernel, moves), in_specs=[HBM] * le...  4.44 us
    unnamed x10, local copies, waits for them, and re-layouts  3.99 us
    all_to_all x1, waiting for transfers between devices, on_device(): tops = lax.all_to_all(top, ('y_lo', 'z', 'core'), 0, 0, tiled=True)  3.82 us
    pallas_call x1, Pallas kernels, open_up(): pl.pallas_call(functools.partial(open_kernel, moves), in_specs=[HBM], out...  2.67 us
    pallas_call x2, Pallas kernels, update(): pl.pallas_call(functools.partial(update_kernel, layer), in_specs=[SCALARS...  2.5 us
  transfers between devices with their start and end apart: 17, of which 6 were waited for; matrix products, arithmetic and copies ran while one was open for 1% of the time, Pallas kernels for 12%

profile of v3, /device:TPU:6, one launch (start us, length us, event | category | flops | bytes accessed | tf_op | source)
XLA Modules:
  0.0 75.1 jit_solution(9834917305797700642)
XLA Ops:
  0.6 2.7 %open.1 = (bf16[128,1152]{1,0:T(8,128)(2,1)}, bf16[128,1152]{1,0:T(8,128)(2,1)}, bf16[2,128,1152]{2,1,0:T(8,128)(2,1)}, f32[1,128]{1,0:T(1,128)S(1)}) custom-call(bf16[2,128,4608]{2,1,0:T(8,128)(2,1)} %bitcast.1), custom_call_target="tpu_custom_call" | custom-call | tf_op jit(solution)/shard_map/open/pallas_call | solution.py:84
  3.3 1.5 %collective-permute-start.4 = (bf16[2,128,1152]{2,1,0:T(8,128)(2,1)}, bf16[2,128,1152]{2,1,0:T(8,128)(2,1)S(1)}, u32[]{:S(2)}, u32[]{:S(2)}) collective-permute-start(bf16[2,128,1152]{2,1,0:T(8,128)(2,1)} %get-tuple-element.23), channel_id=1, source_target_pairs={{0,128},{64,192},{128,0},{192,64},{1,129},{65,193},{129,1},{193,65... | collective-permute-start | bytes 1769480 | tf_op jit(solution)/shard_map/ppermute | solution.py:214
  4.8 2.1 %collective-permute-start = (f32[1,128]{1,0:T(1,128)S(1)}, f32[1,128]{1,0:T(1,128)S(1)}, u32[]{:S(2)}, u32[]{:S(2)}) collective-permute-start(f32[1,128]{1,0:T(1,128)S(1)} %get-tuple-element.20.refs_0_), channel_id=1, source_target_pairs={{0,64},{64,128},{128,192},{192,0},{1,65},{65,129},{129,193},{193,1... | collective-permute-start | bytes 1544 | tf_op jit(solution)/shard_map/ppermute | solution.py:214
  6.9 0.0 collective-permute-start.1
  6.9 2.1 %collective-permute-start.2 = (f32[1,128]{1,0:T(1,128)S(1)}, f32[1,128]{1,0:T(1,128)S(1)}, u32[]{:S(2)}, u32[]{:S(2)}) collective-permute-start(f32[1,128]{1,0:T(1,128)S(1)} %get-tuple-element.20.refs_0_), channel_id=1, source_target_pairs={{0,128},{64,192},{128,0},{192,64},{1,129},{65,193},{129,1},{193,65... | collective-permute-start | bytes 1544 | tf_op jit(solution)/shard_map/ppermute | solution.py:214
  8.9 2.2 %collective-permute-start.10 = (bf16[128,1152]{1,0:T(8,128)(2,1)}, bf16[128,1152]{1,0:T(8,128)(2,1)S(1)}, u32[]{:S(2)}, u32[]{:S(2)}) collective-permute-start(bf16[128,1152]{1,0:T(8,128)(2,1)} %get-tuple-element.29), channel_id=1, source_target_pairs={{0,64},{64,128},{128,192},{192,0},{1,65},{65,129},{129,193},{193,1... | collective-permute-start | bytes 884744 | tf_op jit(solution)/shard_map/ppermute | solution.py:214
  11.1 9.7 %collective-permute-done.refs_1_ = f32[1,128]{1,0:T(1,128)S(1)} collective-permute-done((f32[1,128]{1,0:T(1,128)S(1)}, f32[1,128]{1,0:T(1,128)S(1)}, u32[]{:S(2)}, u32[]{:S(2)}) %collective-permute-start) | collective-permute-done | bytes 544 | tf_op jit(solution)/shard_map/ppermute | solution.py:214
  20.9 0.0 collective-permute-start.11
  20.9 1.9 %load.4 = (bf16[128,1152]{1,0:T(8,128)(2,1)}, bf16[128,1152]{1,0:T(8,128)(2,1)}) custom-call(bf16[2,128,4608]{2,1,0:T(8,128)(2,1)} %bitcast.2), custom_call_target="tpu_custom_call" | custom-call | tf_op jit(solution)/shard_map/load/pallas_call | solution.py:109
  22.8 0.0 collective-permute-done.1.refs_2_
  22.8 3.3 %collective-permute-start.3 = (bf16[128,1152]{1,0:T(8,128)(2,1)}, bf16[128,1152]{1,0:T(8,128)(2,1)S(1)}, u32[]{:S(2)}, u32[]{:S(2)}) collective-permute-start(bf16[128,1152]{1,0:T(8,128)(2,1)} %get-tuple-element.22), channel_id=1, source_target_pairs={{0,64},{64,128},{128,192},{192,0},{1,65},{65,129},{129,193},{193,1... | collective-permute-start | bytes 884744 | tf_op jit(solution)/shard_map/ppermute | solution.py:214
  26.1 0.0 collective-permute-done.2.refs_3_
  26.1 0.0 collective-permute-start.5
  26.1 0.6 meet.1
  26.7 8.6 %all-to-all-start = ((f32[32,1,128]{2,1,0:T(1,128)}), f32[32,1,128]{2,1,0:T(1,128)S(1)}, u32[]{:S(2)}, u32[]{:S(2)}) async-start(f32[32,1,128]{2,1,0:T(1,128)} %meet.1), calls=%async_computation | async-start | bytes 32768 | tf_op jit(solution)/shard_map/all_to_all | solution.py:239
  35.3 0.6 compare_convert_fusion.like_ref
  35.9 1.3 %load.5 = (bf16[128,1152]{1,0:T(8,128)(2,1)S(1)}, bf16[128,1152]{1,0:T(8,128)(2,1)S(1)}, f32[128,1152]{1,0:T(8,128)S(1)}) custom-call(bf16[2,128,4608]{2,1,0:T(8,128)(2,1)} %bitcast.3, bf16[2,128,4608]{2,1,0:T(8,128)(2,1)} %refs_1_.3, f32[2,128,1152]{2,1,0:T(8,128)} %refs_2_.3), custom_call_target="tpu_custom_call" | custom-call | tf_op jit(solution)/shard_map/load/pallas_call | solution.py:109
  37.2 0.0 copy-start
  37.2 0.7 copy-done
  37.9 0.0 copy-start.2
  37.9 0.7 copy-done.2
  38.6 1.3 %load.3 = (bf16[128,1152]{1,0:T(8,128)(2,1)S(1)}, bf16[128,1152]{1,0:T(8,128)(2,1)S(1)}, f32[128,1152]{1,0:T(8,128)S(1)}) custom-call(bf16[2,128,4608]{2,1,0:T(8,128)(2,1)} %bitcast.4, bf16[2,128,4608]{2,1,0:T(8,128)(2,1)} %refs_1_.3, f32[2,128,1152]{2,1,0:T(8,128)} %refs_2_.3), custom_call_target="tpu_custom_call" | custom-call | tf_op jit(solution)/shard_map/load/pallas_call | solution.py:109
  39.9 3.8 %all-to-all-done.top_ref = f32[32,1,128]{2,1,0:T(1,128)S(1)} async-done(((f32[32,1,128]{2,1,0:T(1,128)}), f32[32,1,128]{2,1,0:T(1,128)S(1)}, u32[]{:S(2)}, u32[]{:S(2)}) %all-to-all-start) | async-done | bytes 16416 | tf_op jit(solution)/shard_map/all_to_all | solution.py:239
  43.7 0.0 collective-permute-done.10.refs_1_
  43.7 0.0 collective-permute-done.11.refs_3_
  43.7 0.0 collective-permute-done.4.refs_2_
  43.7 0.0 copy-start.1
  43.7 1.0 %copy-done.1 = bf16[128,1152]{1,0:T(8,128)(2,1)S(1)} copy-done((bf16[128,1152]{1,0:T(8,128)(2,1)S(1)}, bf16[128,1152]{1,0:T(8,128)(2,1)}, u32[]{:S(2)}) %copy-start.1) | copy-done | bytes 294936
  44.7 0.0 copy-start.3
  44.7 1.0 %copy-done.3 = bf16[128,1152]{1,0:T(8,128)(2,1)S(1)} copy-done((bf16[128,1152]{1,0:T(8,128)(2,1)S(1)}, bf16[128,1152]{1,0:T(8,128)(2,1)}, u32[]{:S(2)}) %copy-start.3) | copy-done | bytes 294936
  45.6 0.0 copy-start.4
  45.7 0.7 copy-done.4
  46.3 1.2 %shard_map.51 = (bf16[128,1152]{1,0:T(8,128)(2,1)S(1)}, f32[128,1152]{1,0:T(8,128)S(1)}) custom-call(s32[2]{0:T(128)S(1)} %copy-done.4, f32[32,1,128]{2,1,0:T(1,128)S(1)} %all-to-all-done.top_ref, bf16[128,1152]{1,0:T(8,128)(2,1)S(1)} %copy-done.1, bf16[128,1152]{1,0:T(8,128)(2,1)S(1)} %collective-permute-done.10.refs_1_, ...), custom_call_target="tpu_custom_call" | custom-call | tf_op jit(solution)/shard_map/pallas_call | solution.py:174
  47.6 2.9 %collective-permute-start.12 = (bf16[128,1152]{1,0:T(8,128)(2,1)S(1)}, bf16[128,1152]{1,0:T(8,128)(2,1)S(1)}, u32[]{:S(2)}, u32[]{:S(2)}) collective-permute-start(bf16[128,1152]{1,0:T(8,128)(2,1)S(1)} %get-tuple-element.33.refs_0_), channel_id=1, source_target_pairs={{0,64},{64,128},{128,192},{192,0},{1,65},{65,129},{129,193},{193,1... | collective-permute-start | bytes 884744 | tf_op jit(solution)/shard_map/ppermute | solution.py:214
  50.4 0.0 collective-permute-start.13
  50.4 0.0 collective-permute-done.3.refs_1_
  50.4 0.0 collective-permute-done.5.refs_3_
  50.5 1.3 %shard_map.50 = (bf16[128,1152]{1,0:T(8,128)(2,1)S(1)}, f32[128,1152]{1,0:T(8,128)S(1)}) custom-call(s32[2]{0:T(128)S(1)} %copy-done.4, f32[32,1,128]{2,1,0:T(1,128)S(1)} %all-to-all-done.top_ref, bf16[128,1152]{1,0:T(8,128)(2,1)S(1)} %get-tuple-element.21.refs_0_, bf16[128,1152]{1,0:T(8,128)(2,1)S(1)} %collective-permute-done.3.refs_1_, ...), custom_call_target="tpu_custom_call" | custom-call | tf_op jit(solution)/shard_map/pallas_call | solution.py:174
  51.7 3.3 %collective-permute-start.6 = (bf16[128,1152]{1,0:T(8,128)(2,1)S(1)}, bf16[128,1152]{1,0:T(8,128)(2,1)S(1)}, u32[]{:S(2)}, u32[]{:S(2)}) collective-permute-start(bf16[128,1152]{1,0:T(8,128)(2,1)S(1)} %get-tuple-element.27.refs_3_), channel_id=1, source_target_pairs={{0,64},{64,128},{128,192},{192,0},{1,65},{65,129},{129,193},{193,1... | collective-permute-start | bytes 884744 | tf_op jit(solution)/shard_map/ppermute | solution.py:214
  55.0 0.0 collective-permute-start.8
  55.0 2.8 %collective-permute-done.12.refs_1_ = bf16[128,1152]{1,0:T(8,128)(2,1)S(1)} collective-permute-done((bf16[128,1152]{1,0:T(8,128)(2,1)S(1)}, bf16[128,1152]{1,0:T(8,128)(2,1)S(1)}, u32[]{:S(2)}, u32[]{:S(2)}) %collective-permute-start.12) | collective-permute-done | bytes 294944 | tf_op jit(solution)/shard_map/ppermute | solution.py:214
  57.9 3.8 %collective-permute-start.14 = (bf16[64,1152]{1,0:T(8,128)(2,1)S(1)}, bf16[64,1152]{1,0:T(8,128)(2,1)S(1)}, u32[]{:S(2)}, u32[]{:S(2)}) collective-permute-start(bf16[64,1152]{1,0:T(8,128)(2,1)S(1)} %slice.18), channel_id=1, source_target_pairs={{0,64},{64,128},{128,192},{192,0},{1,65},{65,129},{129,193},{193,1... | collective-permute-start | bytes 442376 | tf_op jit(solution)/shard_map/ppermute | solution.py:214
  61.6 0.0 collective-permute-done.13.refs_2_
  61.6 0.1 collective-permute-start.15
  61.7 2.4 %collective-permute-done.6.refs_4_ = bf16[128,1152]{1,0:T(8,128)(2,1)S(1)} collective-permute-done((bf16[128,1152]{1,0:T(8,128)(2,1)S(1)}, bf16[128,1152]{1,0:T(8,128)(2,1)S(1)}, u32[]{:S(2)}, u32[]{:S(2)}) %collective-permute-start.6) | collective-permute-done | bytes 294944 | tf_op jit(solution)/shard_map/ppermute | solution.py:214
  64.2 3.8 %collective-permute-start.7 = (bf16[64,1152]{1,0:T(8,128)(2,1)S(1)}, bf16[64,1152]{1,0:T(8,128)(2,1)S(1)}, u32[]{:S(2)}, u32[]{:S(2)}) collective-permute-start(bf16[64,1152]{1,0:T(8,128)(2,1)S(1)} %slice.16), channel_id=1, source_target_pairs={{0,64},{64,128},{128,192},{192,0},{1,65},{65,129},{129,193},{193,1... | collective-permute-start | bytes 442376 | tf_op jit(solution)/shard_map/ppermute | solution.py:214
  67.9 0.0 collective-permute-done.8.refs_5_
  68.0 0.1 collective-permute-start.9
  68.1 0.0 collective-permute-done.14.refs_6_
  68.1 1.7 %collective-permute-done.15.refs_7_ = bf16[64,1152]{1,0:T(8,128)(2,1)S(1)} collective-permute-done((bf16[64,1152]{1,0:T(8,128)(2,1)S(1)}, bf16[64,1152]{1,0:T(8,128)(2,1)S(1)}, u32[]{:S(2)}, u32[]{:S(2)}) %collective-permute-start.15) | collective-permute-done | bytes 147488 | tf_op jit(solution)/shard_map/ppermute | solution.py:214
  69.8 1.8 %place.2 = (bf16[2,128,4608]{2,1,0:T(8,128)(2,1)}, f32[2,128,1152]{2,1,0:T(8,128)}) custom-call(bf16[128,1152]{1,0:T(8,128)(2,1)S(1)} %get-tuple-element.33.refs_0_, bf16[128,1152]{1,0:T(8,128)(2,1)S(1)} %collective-permute-done.12.refs_1_, bf16[128,1152]{1,0:T(8,128)(2,1)S(1)} %collective-permute-done.13.refs_2_, ...), custom_call_target="tpu_custom_call" | custom-call | tf_op jit(solution)/shard_map/place/pallas_call | solution.py:201
  71.6 0.0 collective-permute-done.7.refs_0_
  71.6 2.8 %collective-permute-done.9.refs_1_ = bf16[64,1152]{1,0:T(8,128)(2,1)S(1)} collective-permute-done((bf16[64,1152]{1,0:T(8,128)(2,1)S(1)}, bf16[64,1152]{1,0:T(8,128)(2,1)S(1)}, u32[]{:S(2)}, u32[]{:S(2)}) %collective-permute-start.9) | collective-permute-done | bytes 147488 | tf_op jit(solution)/shard_map/ppermute | solution.py:214
  74.4 0.7 place.3
  (4 shorter events, 0.0 us)
Async XLA Ops:
  3.3 40.4 %collective-permute-start.4 = (bf16[2,128,1152]{2,1,0:T(8,128)(2,1)}, bf16[2,128,1152]{2,1,0:T(8,128)(2,1)S(1)}, u32[]{:S(2)}, u32[]{:S(2)}) collective-permute-start(bf16[2,128,1152]{2,1,0:T(8,128)(2,1)} %get-tuple-element.23), channel_id=1, source_target_pairs={{0,128},{64,192},{128,0},{192,64},{1,129},{65,193},{129,1},{193,65... | collective-permute-start | bytes 1769480 | tf_op jit(solution)/shard_map/ppermute | solution.py:214
  4.8 16.1 %collective-permute-start = (f32[1,128]{1,0:T(1,128)S(1)}, f32[1,128]{1,0:T(1,128)S(1)}, u32[]{:S(2)}, u32[]{:S(2)}) collective-permute-start(f32[1,128]{1,0:T(1,128)S(1)} %get-tuple-element.20.refs_0_), channel_id=1, source_target_pairs={{0,64},{64,128},{128,192},{192,0},{1,65},{65,129},{129,193},{193,1... | collective-permute-start | bytes 1544 | tf_op jit(solution)/shard_map/ppermute | solution.py:214
  6.9 15.9 %collective-permute-start.1 = (f32[1,128]{1,0:T(1,128)S(1)}, f32[1,128]{1,0:T(1,128)S(1)}, u32[]{:S(2)}, u32[]{:S(2)}) collective-permute-start(f32[1,128]{1,0:T(1,128)S(1)} %get-tuple-element.20.refs_0_), channel_id=1, source_target_pairs={{0,192},{64,0},{128,64},{192,128},{1,193},{65,1},{129,65},{193,129... | collective-permute-start | bytes 1544 | tf_op jit(solution)/shard_map/ppermute | solution.py:214
  6.9 19.2 %collective-permute-start.2 = (f32[1,128]{1,0:T(1,128)S(1)}, f32[1,128]{1,0:T(1,128)S(1)}, u32[]{:S(2)}, u32[]{:S(2)}) collective-permute-start(f32[1,128]{1,0:T(1,128)S(1)} %get-tuple-element.20.refs_0_), channel_id=1, source_target_pairs={{0,128},{64,192},{128,0},{192,64},{1,129},{65,193},{129,1},{193,65... | collective-permute-start | bytes 1544 | tf_op jit(solution)/shard_map/ppermute | solution.py:214
  8.9 34.8 %collective-permute-start.10 = (bf16[128,1152]{1,0:T(8,128)(2,1)}, bf16[128,1152]{1,0:T(8,128)(2,1)S(1)}, u32[]{:S(2)}, u32[]{:S(2)}) collective-permute-start(bf16[128,1152]{1,0:T(8,128)(2,1)} %get-tuple-element.29), channel_id=1, source_target_pairs={{0,64},{64,128},{128,192},{192,0},{1,65},{65,129},{129,193},{193,1... | collective-permute-start | bytes 884744 | tf_op jit(solution)/shard_map/ppermute | solution.py:214
  20.9 22.8 %collective-permute-start.11 = (bf16[128,1152]{1,0:T(8,128)(2,1)}, bf16[128,1152]{1,0:T(8,128)(2,1)S(1)}, u32[]{:S(2)}, u32[]{:S(2)}) collective-permute-start(bf16[128,1152]{1,0:T(8,128)(2,1)} %get-tuple-element.30), channel_id=1, source_target_pairs={{0,192},{64,0},{128,64},{192,128},{1,193},{65,1},{129,65},{193,129... | collective-permute-start | bytes 884744 | tf_op jit(solution)/shard_map/ppermute | solution.py:214
  22.8 27.7 %collective-permute-start.3 = (bf16[128,1152]{1,0:T(8,128)(2,1)}, bf16[128,1152]{1,0:T(8,128)(2,1)S(1)}, u32[]{:S(2)}, u32[]{:S(2)}) collective-permute-start(bf16[128,1152]{1,0:T(8,128)(2,1)} %get-tuple-element.22), channel_id=1, source_target_pairs={{0,64},{64,128},{128,192},{192,0},{1,65},{65,129},{129,193},{193,1... | collective-permute-start | bytes 884744 | tf_op jit(solution)/shard_map/ppermute | solution.py:214
  26.1 24.3 %collective-permute-start.5 = (bf16[128,1152]{1,0:T(8,128)(2,1)}, bf16[128,1152]{1,0:T(8,128)(2,1)S(1)}, u32[]{:S(2)}, u32[]{:S(2)}) collective-permute-start(bf16[128,1152]{1,0:T(8,128)(2,1)} %get-tuple-element.24), channel_id=1, source_target_pairs={{0,192},{64,0},{128,64},{192,128},{1,193},{65,1},{129,65},{193,129... | collective-permute-start | bytes 884744 | tf_op jit(solution)/shard_map/ppermute | solution.py:214
  26.7 17.0 %all-to-all-start = ((f32[32,1,128]{2,1,0:T(1,128)}), f32[32,1,128]{2,1,0:T(1,128)S(1)}, u32[]{:S(2)}, u32[]{:S(2)}) async-start(f32[32,1,128]{2,1,0:T(1,128)} %meet.1), calls=%async_computation | async-start | bytes 32768 | tf_op jit(solution)/shard_map/all_to_all | solution.py:239
  37.2 0.7 copy-start
  37.9 0.7 copy-start.2
  43.7 1.0 %copy-start.1 = (bf16[128,1152]{1,0:T(8,128)(2,1)S(1)}, bf16[128,1152]{1,0:T(8,128)(2,1)}, u32[]{:S(2)}) copy-start(bf16[128,1152]{1,0:T(8,128)(2,1)} %copy-done) | copy-start | bytes 884740
  44.7 1.0 %copy-start.3 = (bf16[128,1152]{1,0:T(8,128)(2,1)S(1)}, bf16[128,1152]{1,0:T(8,128)(2,1)}, u32[]{:S(2)}) copy-start(bf16[128,1152]{1,0:T(8,128)(2,1)} %copy-done.2) | copy-start | bytes 884740
  45.6 0.7 copy-start.4
  47.6 10.3 %collective-permute-start.12 = (bf16[128,1152]{1,0:T(8,128)(2,1)S(1)}, bf16[128,1152]{1,0:T(8,128)(2,1)S(1)}, u32[]{:S(2)}, u32[]{:S(2)}) collective-permute-start(bf16[128,1152]{1,0:T(8,128)(2,1)S(1)} %get-tuple-element.33.refs_0_), channel_id=1, source_target_pairs={{0,64},{64,128},{128,192},{192,0},{1,65},{65,129},{129,193},{193,1... | collective-permute-start | bytes 884744 | tf_op jit(solution)/shard_map/ppermute | solution.py:214
  50.4 11.2 %collective-permute-start.13 = (bf16[128,1152]{1,0:T(8,128)(2,1)S(1)}, bf16[128,1152]{1,0:T(8,128)(2,1)S(1)}, u32[]{:S(2)}, u32[]{:S(2)}) collective-permute-start(bf16[128,1152]{1,0:T(8,128)(2,1)S(1)} %get-tuple-element.33.refs_0_), channel_id=1, source_target_pairs={{0,192},{64,0},{128,64},{192,128},{1,193},{65,1},{129,65},{193,129... | collective-permute-start | bytes 884744 | tf_op jit(solution)/shard_map/ppermute | solution.py:214
  51.7 12.4 %collective-permute-start.6 = (bf16[128,1152]{1,0:T(8,128)(2,1)S(1)}, bf16[128,1152]{1,0:T(8,128)(2,1)S(1)}, u32[]{:S(2)}, u32[]{:S(2)}) collective-permute-start(bf16[128,1152]{1,0:T(8,128)(2,1)S(1)} %get-tuple-element.27.refs_3_), channel_id=1, source_target_pairs={{0,64},{64,128},{128,192},{192,0},{1,65},{65,129},{129,193},{193,1... | collective-permute-start | bytes 884744 | tf_op jit(solution)/shard_map/ppermute | solution.py:214
  55.0 12.9 %collective-permute-start.8 = (bf16[128,1152]{1,0:T(8,128)(2,1)S(1)}, bf16[128,1152]{1,0:T(8,128)(2,1)S(1)}, u32[]{:S(2)}, u32[]{:S(2)}) collective-permute-start(bf16[128,1152]{1,0:T(8,128)(2,1)S(1)} %get-tuple-element.27.refs_3_), channel_id=1, source_target_pairs={{0,192},{64,0},{128,64},{192,128},{1,193},{65,1},{129,65},{193,129... | collective-permute-start | bytes 884744 | tf_op jit(solution)/shard_map/ppermute | solution.py:214
  57.9 10.2 %collective-permute-start.14 = (bf16[64,1152]{1,0:T(8,128)(2,1)S(1)}, bf16[64,1152]{1,0:T(8,128)(2,1)S(1)}, u32[]{:S(2)}, u32[]{:S(2)}) collective-permute-start(bf16[64,1152]{1,0:T(8,128)(2,1)S(1)} %slice.18), channel_id=1, source_target_pairs={{0,64},{64,128},{128,192},{192,0},{1,65},{65,129},{129,193},{193,1... | collective-permute-start | bytes 442376 | tf_op jit(solution)/shard_map/ppermute | solution.py:214
  61.6 8.1 %collective-permute-start.15 = (bf16[64,1152]{1,0:T(8,128)(2,1)S(1)}, bf16[64,1152]{1,0:T(8,128)(2,1)S(1)}, u32[]{:S(2)}, u32[]{:S(2)}) collective-permute-start(bf16[64,1152]{1,0:T(8,128)(2,1)S(1)} %slice.19), channel_id=1, source_target_pairs={{0,192},{64,0},{128,64},{192,128},{1,193},{65,1},{129,65},{193,129... | collective-permute-start | bytes 442376 | tf_op jit(solution)/shard_map/ppermute | solution.py:214
  64.2 7.4 %collective-permute-start.7 = (bf16[64,1152]{1,0:T(8,128)(2,1)S(1)}, bf16[64,1152]{1,0:T(8,128)(2,1)S(1)}, u32[]{:S(2)}, u32[]{:S(2)}) collective-permute-start(bf16[64,1152]{1,0:T(8,128)(2,1)S(1)} %slice.16), channel_id=1, source_target_pairs={{0,64},{64,128},{128,192},{192,0},{1,65},{65,129},{129,193},{193,1... | collective-permute-start | bytes 442376 | tf_op jit(solution)/shard_map/ppermute | solution.py:214
  68.0 6.4 %collective-permute-start.9 = (bf16[64,1152]{1,0:T(8,128)(2,1)S(1)}, bf16[64,1152]{1,0:T(8,128)(2,1)S(1)}, u32[]{:S(2)}, u32[]{:S(2)}) collective-permute-start(bf16[64,1152]{1,0:T(8,128)(2,1)S(1)} %slice.17), channel_id=1, source_target_pairs={{0,192},{64,0},{128,64},{192,128},{1,193},{65,1},{129,65},{193,129... | collective-permute-start | bytes 442376 | tf_op jit(solution)/shard_map/ppermute | solution.py:214

commit v4 on v3

--- a/solution.py
+++ b/solution.py
@@ -15,6 +15,7 @@
 AXES = ("rep", *FSDP)
 SIZES = (4, 2, 2, 8, 2)
 REP = 4
+PIECES = 4
 
 clip_share = 0.5
 peak_eps = 1e-06
@@ -187,8 +188,11 @@
         src = refs[k]
         owned = src.shape[-1]
         here = columns(back, owned) if which == 0 else pl.ds(0, owned)
-        dst = outs[which].at[layer, pl.ds(first, height), here]
-        copies.append(pltpu.make_async_copy(src, dst, sems.at[k]))
+        step = height // PIECES
+        for part in range(PIECES):
+            dst = outs[which].at[layer, pl.ds(first + part * step, step), here]
+            rows = src.at[pl.ds(part * step, step)]
+            copies.append(pltpu.make_async_copy(rows, dst, sems.at[k * PIECES + part]))
     run_all(copies)
 
 
@@ -203,7 +207,7 @@
         in_specs=[WHOLE] * len(pieces) + [HBM] * len(aliases),
         out_specs=[HBM] * len(shapes),
         out_shape=shapes,
-        scratch_shapes=[pltpu.SemaphoreType.DMA((len(moves),))],
+        scratch_shapes=[pltpu.SemaphoreType.DMA((len(moves) * PIECES,))],
         input_output_aliases=aliases,
         compiler_params=SMALL,
         name="place",

time: 75.4 us -> 75.5 us (level)
  transfers between devices with their start and end apart: 17 -> 17, of which waited for: 6 -> 6; matrix products, arithmetic and copies ran while one was open for 1% -> 1% of each run, Pallas kernels for 12% -> 13%
where the time goes in v4:
time: 75.5 us; the launch traced here: 75.2 us
  starting transfers between devices  33.6 us (45%)
  waiting for transfers between devices  23.1 us (31%)
  Pallas kernels  13 us (17%)
  local copies, waits for them, and re-layouts  4.04 us (5%)
  between operations  0.79 us (1%)
    ppermute x16, starting transfers between devices, shift(): return lax.ppermute(value, 'rep', [(i, (i + by) % REP) for i in range(REP)])  25 us
    ppermute x16, waiting for transfers between devices, shift(): return lax.ppermute(value, 'rep', [(i, (i + by) % REP) for i in range(REP)])  19.3 us
    all_to_all x1, starting transfers between devices, on_device(): tops = lax.all_to_all(top, ('y_lo', 'z', 'core'), 0, 0, tiled=True)  8.6 us
    pallas_call x3, Pallas kernels, load(): pl.pallas_call(functools.partial(load_kernel, moves), in_specs=[HBM] * le...  4.44 us
    unnamed x10, local copies, waits for them, and re-layouts  3.99 us
    all_to_all x1, waiting for transfers between devices, on_device(): tops = lax.all_to_all(top, ('y_lo', 'z', 'core'), 0, 0, tiled=True)  3.82 us
    pallas_call x2, Pallas kernels, place(): pl.pallas_call(functools.partial(place_kernel, moves, len(shapes)), in_sp...  2.81 us
    pallas_call x1, Pallas kernels, open_up(): pl.pallas_call(functools.partial(open_kernel, moves), in_specs=[HBM], out...  2.67 us
  transfers between devices with their start and end apart: 17, of which 6 were waited for; matrix products, arithmetic and copies ran while one was open for 1% of the time, Pallas kernels for 13%

profile of v4, /device:TPU:6, one launch (start us, length us, event | category | flops | bytes accessed | tf_op | source)
XLA Modules:
  0.0 75.2 jit_solution(5106376931086253686)
XLA Ops:
  0.6 2.7 %open.1 = (bf16[128,1152]{1,0:T(8,128)(2,1)}, bf16[128,1152]{1,0:T(8,128)(2,1)}, bf16[2,128,1152]{2,1,0:T(8,128)(2,1)}, f32[1,128]{1,0:T(1,128)S(1)}) custom-call(bf16[2,128,4608]{2,1,0:T(8,128)(2,1)} %bitcast.1), custom_call_target="tpu_custom_call" | custom-call | tf_op jit(solution)/shard_map/open/pallas_call | solution.py:85
  3.3 1.5 %collective-permute-start.4 = (bf16[2,128,1152]{2,1,0:T(8,128)(2,1)}, bf16[2,128,1152]{2,1,0:T(8,128)(2,1)S(1)}, u32[]{:S(2)}, u32[]{:S(2)}) collective-permute-start(bf16[2,128,1152]{2,1,0:T(8,128)(2,1)} %get-tuple-element.23), channel_id=1, source_target_pairs={{0,128},{64,192},{128,0},{192,64},{1,129},{65,193},{129,1},{193,65... | collective-permute-start | bytes 1769480 | tf_op jit(solution)/shard_map/ppermute | solution.py:218
  4.8 2.1 %collective-permute-start = (f32[1,128]{1,0:T(1,128)S(1)}, f32[1,128]{1,0:T(1,128)S(1)}, u32[]{:S(2)}, u32[]{:S(2)}) collective-permute-start(f32[1,128]{1,0:T(1,128)S(1)} %get-tuple-element.20.refs_0_), channel_id=1, source_target_pairs={{0,64},{64,128},{128,192},{192,0},{1,65},{65,129},{129,193},{193,1... | collective-permute-start | bytes 1544 | tf_op jit(solution)/shard_map/ppermute | solution.py:218
  6.9 0.0 collective-permute-start.1
  6.9 2.1 %collective-permute-start.2 = (f32[1,128]{1,0:T(1,128)S(1)}, f32[1,128]{1,0:T(1,128)S(1)}, u32[]{:S(2)}, u32[]{:S(2)}) collective-permute-start(f32[1,128]{1,0:T(1,128)S(1)} %get-tuple-element.20.refs_0_), channel_id=1, source_target_pairs={{0,128},{64,192},{128,0},{192,64},{1,129},{65,193},{129,1},{193,65... | collective-permute-start | bytes 1544 | tf_op jit(solution)/shard_map/ppermute | solution.py:218
  8.9 2.2 %collective-permute-start.10 = (bf16[128,1152]{1,0:T(8,128)(2,1)}, bf16[128,1152]{1,0:T(8,128)(2,1)S(1)}, u32[]{:S(2)}, u32[]{:S(2)}) collective-permute-start(bf16[128,1152]{1,0:T(8,128)(2,1)} %get-tuple-element.29), channel_id=1, source_target_pairs={{0,64},{64,128},{128,192},{192,0},{1,65},{65,129},{129,193},{193,1... | collective-permute-start | bytes 884744 | tf_op jit(solution)/shard_map/ppermute | solution.py:218
  11.1 9.7 %collective-permute-done.refs_1_ = f32[1,128]{1,0:T(1,128)S(1)} collective-permute-done((f32[1,128]{1,0:T(1,128)S(1)}, f32[1,128]{1,0:T(1,128)S(1)}, u32[]{:S(2)}, u32[]{:S(2)}) %collective-permute-start) | collective-permute-done | bytes 544 | tf_op jit(solution)/shard_map/ppermute | solution.py:218
  20.9 0.0 collective-permute-start.11
  20.9 1.9 %load.4 = (bf16[128,1152]{1,0:T(8,128)(2,1)}, bf16[128,1152]{1,0:T(8,128)(2,1)}) custom-call(bf16[2,128,4608]{2,1,0:T(8,128)(2,1)} %bitcast.2), custom_call_target="tpu_custom_call" | custom-call | tf_op jit(solution)/shard_map/load/pallas_call | solution.py:110
  22.8 0.0 collective-permute-done.1.refs_2_
  22.8 3.3 %collective-permute-start.3 = (bf16[128,1152]{1,0:T(8,128)(2,1)}, bf16[128,1152]{1,0:T(8,128)(2,1)S(1)}, u32[]{:S(2)}, u32[]{:S(2)}) collective-permute-start(bf16[128,1152]{1,0:T(8,128)(2,1)} %get-tuple-element.22), channel_id=1, source_target_pairs={{0,64},{64,128},{128,192},{192,0},{1,65},{65,129},{129,193},{193,1... | collective-permute-start | bytes 884744 | tf_op jit(solution)/shard_map/ppermute | solution.py:218
  26.1 0.0 collective-permute-done.2.refs_3_
  26.1 0.0 collective-permute-start.5
  26.1 0.6 meet.1
  26.7 8.6 %all-to-all-start = ((f32[32,1,128]{2,1,0:T(1,128)}), f32[32,1,128]{2,1,0:T(1,128)S(1)}, u32[]{:S(2)}, u32[]{:S(2)}) async-start(f32[32,1,128]{2,1,0:T(1,128)} %meet.1), calls=%async_computation | async-start | bytes 32768 | tf_op jit(solution)/shard_map/all_to_all | solution.py:243
  35.3 0.6 compare_convert_fusion.like_ref
  35.9 1.3 %load.5 = (bf16[128,1152]{1,0:T(8,128)(2,1)S(1)}, bf16[128,1152]{1,0:T(8,128)(2,1)S(1)}, f32[128,1152]{1,0:T(8,128)S(1)}) custom-call(bf16[2,128,4608]{2,1,0:T(8,128)(2,1)} %bitcast.3, bf16[2,128,4608]{2,1,0:T(8,128)(2,1)} %refs_1_.3, f32[2,128,1152]{2,1,0:T(8,128)} %refs_2_.3), custom_call_target="tpu_custom_call" | custom-call | tf_op jit(solution)/shard_map/load/pallas_call | solution.py:110
  37.2 0.0 copy-start
  37.2 0.7 copy-done
  37.9 0.0 copy-start.2
  37.9 0.7 copy-done.2
  38.6 1.3 %load.3 = (bf16[128,1152]{1,0:T(8,128)(2,1)S(1)}, bf16[128,1152]{1,0:T(8,128)(2,1)S(1)}, f32[128,1152]{1,0:T(8,128)S(1)}) custom-call(bf16[2,128,4608]{2,1,0:T(8,128)(2,1)} %bitcast.4, bf16[2,128,4608]{2,1,0:T(8,128)(2,1)} %refs_1_.3, f32[2,128,1152]{2,1,0:T(8,128)} %refs_2_.3), custom_call_target="tpu_custom_call" | custom-call | tf_op jit(solution)/shard_map/load/pallas_call | solution.py:110
  39.9 3.8 %all-to-all-done.top_ref = f32[32,1,128]{2,1,0:T(1,128)S(1)} async-done(((f32[32,1,128]{2,1,0:T(1,128)}), f32[32,1,128]{2,1,0:T(1,128)S(1)}, u32[]{:S(2)}, u32[]{:S(2)}) %all-to-all-start) | async-done | bytes 16416 | tf_op jit(solution)/shard_map/all_to_all | solution.py:243
  43.7 0.0 collective-permute-done.10.refs_1_
  43.7 0.0 collective-permute-done.11.refs_3_
  43.7 0.0 collective-permute-done.4.refs_2_
  43.7 0.0 copy-start.1
  43.7 1.0 %copy-done.1 = bf16[128,1152]{1,0:T(8,128)(2,1)S(1)} copy-done((bf16[128,1152]{1,0:T(8,128)(2,1)S(1)}, bf16[128,1152]{1,0:T(8,128)(2,1)}, u32[]{:S(2)}) %copy-start.1) | copy-done | bytes 294936
  44.7 0.0 copy-start.3
  44.7 1.0 %copy-done.3 = bf16[128,1152]{1,0:T(8,128)(2,1)S(1)} copy-done((bf16[128,1152]{1,0:T(8,128)(2,1)S(1)}, bf16[128,1152]{1,0:T(8,128)(2,1)}, u32[]{:S(2)}) %copy-start.3) | copy-done | bytes 294936
  45.6 0.0 copy-start.4
  45.7 0.7 copy-done.4
  46.3 1.2 %shard_map.51 = (bf16[128,1152]{1,0:T(8,128)(2,1)S(1)}, f32[128,1152]{1,0:T(8,128)S(1)}) custom-call(s32[2]{0:T(128)S(1)} %copy-done.4, f32[32,1,128]{2,1,0:T(1,128)S(1)} %all-to-all-done.top_ref, bf16[128,1152]{1,0:T(8,128)(2,1)S(1)} %copy-done.1, bf16[128,1152]{1,0:T(8,128)(2,1)S(1)} %collective-permute-done.10.refs_1_, ...), custom_call_target="tpu_custom_call" | custom-call | tf_op jit(solution)/shard_map/pallas_call | solution.py:175
  47.6 2.9 %collective-permute-start.12 = (bf16[128,1152]{1,0:T(8,128)(2,1)S(1)}, bf16[128,1152]{1,0:T(8,128)(2,1)S(1)}, u32[]{:S(2)}, u32[]{:S(2)}) collective-permute-start(bf16[128,1152]{1,0:T(8,128)(2,1)S(1)} %get-tuple-element.33.refs_0_), channel_id=1, source_target_pairs={{0,64},{64,128},{128,192},{192,0},{1,65},{65,129},{129,193},{193,1... | collective-permute-start | bytes 884744 | tf_op jit(solution)/shard_map/ppermute | solution.py:218
  50.4 0.0 collective-permute-start.13
  50.4 0.0 collective-permute-done.3.refs_1_
  50.4 0.0 collective-permute-done.5.refs_3_
  50.5 1.3 %shard_map.50 = (bf16[128,1152]{1,0:T(8,128)(2,1)S(1)}, f32[128,1152]{1,0:T(8,128)S(1)}) custom-call(s32[2]{0:T(128)S(1)} %copy-done.4, f32[32,1,128]{2,1,0:T(1,128)S(1)} %all-to-all-done.top_ref, bf16[128,1152]{1,0:T(8,128)(2,1)S(1)} %get-tuple-element.21.refs_0_, bf16[128,1152]{1,0:T(8,128)(2,1)S(1)} %collective-permute-done.3.refs_1_, ...), custom_call_target="tpu_custom_call" | custom-call | tf_op jit(solution)/shard_map/pallas_call | solution.py:175
  51.7 3.3 %collective-permute-start.6 = (bf16[128,1152]{1,0:T(8,128)(2,1)S(1)}, bf16[128,1152]{1,0:T(8,128)(2,1)S(1)}, u32[]{:S(2)}, u32[]{:S(2)}) collective-permute-start(bf16[128,1152]{1,0:T(8,128)(2,1)S(1)} %get-tuple-element.27.refs_3_), channel_id=1, source_target_pairs={{0,64},{64,128},{128,192},{192,0},{1,65},{65,129},{129,193},{193,1... | collective-permute-start | bytes 884744 | tf_op jit(solution)/shard_map/ppermute | solution.py:218
  55.0 0.0 collective-permute-start.8
  55.0 2.8 %collective-permute-done.12.refs_1_ = bf16[128,1152]{1,0:T(8,128)(2,1)S(1)} collective-permute-done((bf16[128,1152]{1,0:T(8,128)(2,1)S(1)}, bf16[128,1152]{1,0:T(8,128)(2,1)S(1)}, u32[]{:S(2)}, u32[]{:S(2)}) %collective-permute-start.12) | collective-permute-done | bytes 294944 | tf_op jit(solution)/shard_map/ppermute | solution.py:218
  57.9 3.8 %collective-permute-start.14 = (bf16[64,1152]{1,0:T(8,128)(2,1)S(1)}, bf16[64,1152]{1,0:T(8,128)(2,1)S(1)}, u32[]{:S(2)}, u32[]{:S(2)}) collective-permute-start(bf16[64,1152]{1,0:T(8,128)(2,1)S(1)} %slice.18), channel_id=1, source_target_pairs={{0,64},{64,128},{128,192},{192,0},{1,65},{65,129},{129,193},{193,1... | collective-permute-start | bytes 442376 | tf_op jit(solution)/shard_map/ppermute | solution.py:218
  61.6 0.0 collective-permute-done.13.refs_2_
  61.6 0.1 collective-permute-start.15
  61.7 2.4 %collective-permute-done.6.refs_4_ = bf16[128,1152]{1,0:T(8,128)(2,1)S(1)} collective-permute-done((bf16[128,1152]{1,0:T(8,128)(2,1)S(1)}, bf16[128,1152]{1,0:T(8,128)(2,1)S(1)}, u32[]{:S(2)}, u32[]{:S(2)}) %collective-permute-start.6) | collective-permute-done | bytes 294944 | tf_op jit(solution)/shard_map/ppermute | solution.py:218
  64.2 3.8 %collective-permute-start.7 = (bf16[64,1152]{1,0:T(8,128)(2,1)S(1)}, bf16[64,1152]{1,0:T(8,128)(2,1)S(1)}, u32[]{:S(2)}, u32[]{:S(2)}) collective-permute-start(bf16[64,1152]{1,0:T(8,128)(2,1)S(1)} %slice.16), channel_id=1, source_target_pairs={{0,64},{64,128},{128,192},{192,0},{1,65},{65,129},{129,193},{193,1... | collective-permute-start | bytes 442376 | tf_op jit(solution)/shard_map/ppermute | solution.py:218
  67.9 0.0 collective-permute-done.8.refs_5_
  68.0 0.1 collective-permute-start.9
  68.1 0.0 collective-permute-done.14.refs_6_
  68.1 1.7 %collective-permute-done.15.refs_7_ = bf16[64,1152]{1,0:T(8,128)(2,1)S(1)} collective-permute-done((bf16[64,1152]{1,0:T(8,128)(2,1)S(1)}, bf16[64,1152]{1,0:T(8,128)(2,1)S(1)}, u32[]{:S(2)}, u32[]{:S(2)}) %collective-permute-start.15) | collective-permute-done | bytes 147488 | tf_op jit(solution)/shard_map/ppermute | solution.py:218
  69.8 2.0 %place.2 = (bf16[2,128,4608]{2,1,0:T(8,128)(2,1)}, f32[2,128,1152]{2,1,0:T(8,128)}) custom-call(bf16[128,1152]{1,0:T(8,128)(2,1)S(1)} %get-tuple-element.33.refs_0_, bf16[128,1152]{1,0:T(8,128)(2,1)S(1)} %collective-permute-done.12.refs_1_, bf16[128,1152]{1,0:T(8,128)(2,1)S(1)} %collective-permute-done.13.refs_2_, ...), custom_call_target="tpu_custom_call" | custom-call | tf_op jit(solution)/shard_map/place/pallas_call | solution.py:205
  71.8 0.0 collective-permute-done.7.refs_0_
  71.8 2.6 %collective-permute-done.9.refs_1_ = bf16[64,1152]{1,0:T(8,128)(2,1)S(1)} collective-permute-done((bf16[64,1152]{1,0:T(8,128)(2,1)S(1)}, bf16[64,1152]{1,0:T(8,128)(2,1)S(1)}, u32[]{:S(2)}, u32[]{:S(2)}) %collective-permute-start.9) | collective-permute-done | bytes 147488 | tf_op jit(solution)/shard_map/ppermute | solution.py:218
  74.4 0.8 %place.3 = bf16[2,128,4608]{2,1,0:T(8,128)(2,1)} custom-call(bf16[64,1152]{1,0:T(8,128)(2,1)S(1)} %collective-permute-done.7.refs_0_, bf16[64,1152]{1,0:T(8,128)(2,1)S(1)} %collective-permute-done.9.refs_1_, bf16[2,128,4608]{2,1,0:T(8,128)(2,1)} %get-tuple-element.36.refs_2_), custom_call_target="tpu_custom_call", output_to_operand_aliasing={{}: (2, {})} | custom-call | tf_op jit(solution)/shard_map/place/pallas_call | solution.py:205
  (4 shorter events, 0.0 us)
Async XLA Ops:
  3.3 40.4 %collective-permute-start.4 = (bf16[2,128,1152]{2,1,0:T(8,128)(2,1)}, bf16[2,128,1152]{2,1,0:T(8,128)(2,1)S(1)}, u32[]{:S(2)}, u32[]{:S(2)}) collective-permute-start(bf16[2,128,1152]{2,1,0:T(8,128)(2,1)} %get-tuple-element.23), channel_id=1, source_target_pairs={{0,128},{64,192},{128,0},{192,64},{1,129},{65,193},{129,1},{193,65... | collective-permute-start | bytes 1769480 | tf_op jit(solution)/shard_map/ppermute | solution.py:218
  4.8 16.1 %collective-permute-start = (f32[1,128]{1,0:T(1,128)S(1)}, f32[1,128]{1,0:T(1,128)S(1)}, u32[]{:S(2)}, u32[]{:S(2)}) collective-permute-start(f32[1,128]{1,0:T(1,128)S(1)} %get-tuple-element.20.refs_0_), channel_id=1, source_target_pairs={{0,64},{64,128},{128,192},{192,0},{1,65},{65,129},{129,193},{193,1... | collective-permute-start | bytes 1544 | tf_op jit(solution)/shard_map/ppermute | solution.py:218
  6.9 15.9 %collective-permute-start.1 = (f32[1,128]{1,0:T(1,128)S(1)}, f32[1,128]{1,0:T(1,128)S(1)}, u32[]{:S(2)}, u32[]{:S(2)}) collective-permute-start(f32[1,128]{1,0:T(1,128)S(1)} %get-tuple-element.20.refs_0_), channel_id=1, source_target_pairs={{0,192},{64,0},{128,64},{192,128},{1,193},{65,1},{129,65},{193,129... | collective-permute-start | bytes 1544 | tf_op jit(solution)/shard_map/ppermute | solution.py:218
  6.9 19.2 %collective-permute-start.2 = (f32[1,128]{1,0:T(1,128)S(1)}, f32[1,128]{1,0:T(1,128)S(1)}, u32[]{:S(2)}, u32[]{:S(2)}) collective-permute-start(f32[1,128]{1,0:T(1,128)S(1)} %get-tuple-element.20.refs_0_), channel_id=1, source_target_pairs={{0,128},{64,192},{128,0},{192,64},{1,129},{65,193},{129,1},{193,65... | collective-permute-start | bytes 1544 | tf_op jit(solution)/shard_map/ppermute | solution.py:218
  8.9 34.8 %collective-permute-start.10 = (bf16[128,1152]{1,0:T(8,128)(2,1)}, bf16[128,1152]{1,0:T(8,128)(2,1)S(1)}, u32[]{:S(2)}, u32[]{:S(2)}) collective-permute-start(bf16[128,1152]{1,0:T(8,128)(2,1)} %get-tuple-element.29), channel_id=1, source_target_pairs={{0,64},{64,128},{128,192},{192,0},{1,65},{65,129},{129,193},{193,1... | collective-permute-start | bytes 884744 | tf_op jit(solution)/shard_map/ppermute | solution.py:218
  20.9 22.8 %collective-permute-start.11 = (bf16[128,1152]{1,0:T(8,128)(2,1)}, bf16[128,1152]{1,0:T(8,128)(2,1)S(1)}, u32[]{:S(2)}, u32[]{:S(2)}) collective-permute-start(bf16[128,1152]{1,0:T(8,128)(2,1)} %get-tuple-element.30), channel_id=1, source_target_pairs={{0,192},{64,0},{128,64},{192,128},{1,193},{65,1},{129,65},{193,129... | collective-permute-start | bytes 884744 | tf_op jit(solution)/shard_map/ppermute | solution.py:218
  22.8 27.7 %collective-permute-start.3 = (bf16[128,1152]{1,0:T(8,128)(2,1)}, bf16[128,1152]{1,0:T(8,128)(2,1)S(1)}, u32[]{:S(2)}, u32[]{:S(2)}) collective-permute-start(bf16[128,1152]{1,0:T(8,128)(2,1)} %get-tuple-element.22), channel_id=1, source_target_pairs={{0,64},{64,128},{128,192},{192,0},{1,65},{65,129},{129,193},{193,1... | collective-permute-start | bytes 884744 | tf_op jit(solution)/shard_map/ppermute | solution.py:218
  26.1 24.3 %collective-permute-start.5 = (bf16[128,1152]{1,0:T(8,128)(2,1)}, bf16[128,1152]{1,0:T(8,128)(2,1)S(1)}, u32[]{:S(2)}, u32[]{:S(2)}) collective-permute-start(bf16[128,1152]{1,0:T(8,128)(2,1)} %get-tuple-element.24), channel_id=1, source_target_pairs={{0,192},{64,0},{128,64},{192,128},{1,193},{65,1},{129,65},{193,129... | collective-permute-start | bytes 884744 | tf_op jit(solution)/shard_map/ppermute | solution.py:218
  26.7 17.0 %all-to-all-start = ((f32[32,1,128]{2,1,0:T(1,128)}), f32[32,1,128]{2,1,0:T(1,128)S(1)}, u32[]{:S(2)}, u32[]{:S(2)}) async-start(f32[32,1,128]{2,1,0:T(1,128)} %meet.1), calls=%async_computation | async-start | bytes 32768 | tf_op jit(solution)/shard_map/all_to_all | solution.py:243
  37.2 0.7 copy-start
  37.9 0.7 copy-start.2
  43.7 1.0 %copy-start.1 = (bf16[128,1152]{1,0:T(8,128)(2,1)S(1)}, bf16[128,1152]{1,0:T(8,128)(2,1)}, u32[]{:S(2)}) copy-start(bf16[128,1152]{1,0:T(8,128)(2,1)} %copy-done) | copy-start | bytes 884740
  44.7 1.0 %copy-start.3 = (bf16[128,1152]{1,0:T(8,128)(2,1)S(1)}, bf16[128,1152]{1,0:T(8,128)(2,1)}, u32[]{:S(2)}) copy-start(bf16[128,1152]{1,0:T(8,128)(2,1)} %copy-done.2) | copy-start | bytes 884740
  45.6 0.7 copy-start.4
  47.6 10.3 %collective-permute-start.12 = (bf16[128,1152]{1,0:T(8,128)(2,1)S(1)}, bf16[128,1152]{1,0:T(8,128)(2,1)S(1)}, u32[]{:S(2)}, u32[]{:S(2)}) collective-permute-start(bf16[128,1152]{1,0:T(8,128)(2,1)S(1)} %get-tuple-element.33.refs_0_), channel_id=1, source_target_pairs={{0,64},{64,128},{128,192},{192,0},{1,65},{65,129},{129,193},{193,1... | collective-permute-start | bytes 884744 | tf_op jit(solution)/shard_map/ppermute | solution.py:218
  50.4 11.2 %collective-permute-start.13 = (bf16[128,1152]{1,0:T(8,128)(2,1)S(1)}, bf16[128,1152]{1,0:T(8,128)(2,1)S(1)}, u32[]{:S(2)}, u32[]{:S(2)}) collective-permute-start(bf16[128,1152]{1,0:T(8,128)(2,1)S(1)} %get-tuple-element.33.refs_0_), channel_id=1, source_target_pairs={{0,192},{64,0},{128,64},{192,128},{1,193},{65,1},{129,65},{193,129... | collective-permute-start | bytes 884744 | tf_op jit(solution)/shard_map/ppermute | solution.py:218
  51.7 12.4 %collective-permute-start.6 = (bf16[128,1152]{1,0:T(8,128)(2,1)S(1)}, bf16[128,1152]{1,0:T(8,128)(2,1)S(1)}, u32[]{:S(2)}, u32[]{:S(2)}) collective-permute-start(bf16[128,1152]{1,0:T(8,128)(2,1)S(1)} %get-tuple-element.27.refs_3_), channel_id=1, source_target_pairs={{0,64},{64,128},{128,192},{192,0},{1,65},{65,129},{129,193},{193,1... | collective-permute-start | bytes 884744 | tf_op jit(solution)/shard_map/ppermute | solution.py:218
  55.0 12.9 %collective-permute-start.8 = (bf16[128,1152]{1,0:T(8,128)(2,1)S(1)}, bf16[128,1152]{1,0:T(8,128)(2,1)S(1)}, u32[]{:S(2)}, u32[]{:S(2)}) collective-permute-start(bf16[128,1152]{1,0:T(8,128)(2,1)S(1)} %get-tuple-element.27.refs_3_), channel_id=1, source_target_pairs={{0,192},{64,0},{128,64},{192,128},{1,193},{65,1},{129,65},{193,129... | collective-permute-start | bytes 884744 | tf_op jit(solution)/shard_map/ppermute | solution.py:218
  57.9 10.2 %collective-permute-start.14 = (bf16[64,1152]{1,0:T(8,128)(2,1)S(1)}, bf16[64,1152]{1,0:T(8,128)(2,1)S(1)}, u32[]{:S(2)}, u32[]{:S(2)}) collective-permute-start(bf16[64,1152]{1,0:T(8,128)(2,1)S(1)} %slice.18), channel_id=1, source_target_pairs={{0,64},{64,128},{128,192},{192,0},{1,65},{65,129},{129,193},{193,1... | collective-permute-start | bytes 442376 | tf_op jit(solution)/shard_map/ppermute | solution.py:218
  61.6 8.1 %collective-permute-start.15 = (bf16[64,1152]{1,0:T(8,128)(2,1)S(1)}, bf16[64,1152]{1,0:T(8,128)(2,1)S(1)}, u32[]{:S(2)}, u32[]{:S(2)}) collective-permute-start(bf16[64,1152]{1,0:T(8,128)(2,1)S(1)} %slice.19), channel_id=1, source_target_pairs={{0,192},{64,0},{128,64},{192,128},{1,193},{65,1},{129,65},{193,129... | collective-permute-start | bytes 442376 | tf_op jit(solution)/shard_map/ppermute | solution.py:218
  64.2 7.7 %collective-permute-start.7 = (bf16[64,1152]{1,0:T(8,128)(2,1)S(1)}, bf16[64,1152]{1,0:T(8,128)(2,1)S(1)}, u32[]{:S(2)}, u32[]{:S(2)}) collective-permute-start(bf16[64,1152]{1,0:T(8,128)(2,1)S(1)} %slice.16), channel_id=1, source_target_pairs={{0,64},{64,128},{128,192},{192,0},{1,65},{65,129},{129,193},{193,1... | collective-permute-start | bytes 442376 | tf_op jit(solution)/shard_map/ppermute | solution.py:218
  68.0 6.4 %collective-permute-start.9 = (bf16[64,1152]{1,0:T(8,128)(2,1)S(1)}, bf16[64,1152]{1,0:T(8,128)(2,1)S(1)}, u32[]{:S(2)}, u32[]{:S(2)}) collective-permute-start(bf16[64,1152]{1,0:T(8,128)(2,1)S(1)} %slice.17), channel_id=1, source_target_pairs={{0,192},{64,0},{128,64},{192,128},{1,193},{65,1},{129,65},{193,129... | collective-permute-start | bytes 442376 | tf_op jit(solution)/shard_map/ppermute | solution.py:218
